TPU v7x, 32 devices: a whole 2x2x4 slice. The times are simulated.
32 devices in a mesh: dp: 4 (over y, x), expert: 8 (over z, core).
Axes of the slice: x: 2, y: 2, z: 4, core: 2. Of those that a mesh axis runs over, the one named last changes fastest.
Arguments:
- tokens: bfloat16 [4096, 2048], P(('dp', 'expert')), may hold values from -6 to 6
- routes: int32 [4096, 8], P(('dp', 'expert')), may hold values from 0 to 15, all different within a row
- route_weight: float32 [4096, 8], P(('dp', 'expert')), may hold values from 0.05 to 0.5
- bias: float32 [16], replicated, may hold values from -3 to 3
- w_gate: bfloat16 [16, 768, 2048], P('expert', 'dp'), may hold values from -0.125 to 0.125
- w_up: bfloat16 [16, 768, 2048], P('expert', 'dp'), may hold values from -0.125 to 0.125
- w_down: bfloat16 [16, 768, 2048], P('expert', 'dp'), may hold values from -0.21875 to 0.21875
Outputs:
- mixed: bfloat16 [4096, 2048], P(('dp', 'expert'))
- new_bias: float32 [16], replicated
- counts: int32 [16], replicated
Inputs may be any that keep to these rules, and one draw needn't show every extreme that they name: `routes`: each token names 8 different experts.
All inputs are finite; a program needn't handle non-finite values.
Results may differ from a plain program's by a relative error of at most 0.0057.
Values may be sent and summed in bfloat16 or wider, within the bound.
A program may use at most 128 MiB of HBM per device.

v0:
```python
import functools

import jax
import jax.numpy as jnp
from jax import lax
from jax.experimental import pallas as pl
from jax.experimental.pallas import tpu as pltpu
from jax.sharding import PartitionSpec as P

bias_rate = 0.05
MESH = pl.DeviceIdType.MESH
VMEM_BYTES = 67043328
chunks = 8


def expert_products(received, gate_w, up_w, down_w):
    gate_act = jnp.einsum("sjcd,jfd->sjcf", received, gate_w, preferred_element_type=jnp.float32)
    up_act = jnp.einsum("sjcd,jfd->sjcf", received, up_w, preferred_element_type=jnp.float32)
    hidden = (jax.nn.silu(gate_act) * up_act).astype(jnp.bfloat16)
    return jnp.einsum("sjcf,jfd->sjcd", hidden, down_w, preferred_element_type=jnp.float32)


def exchange_body(tokens, routes, route_weight, bias, w_gate, w_up, w_down):
    tok_rows, feature_width = tokens.shape
    top_count = routes.shape[1]
    experts = bias.shape[0]
    groups = lax.axis_size("expert")
    per_device = w_gate.shape[0]
    capacity = 5 * tok_rows * top_count // (4 * experts)
    flat_routes = routes.reshape(-1)
    labels = jnp.arange(experts, dtype=jnp.int32)
    picked = (flat_routes[:, None] == labels[None, :]).astype(jnp.int32)
    running = jnp.cumsum(picked, axis=0) - picked
    slot_rank = jnp.sum(running * picked, axis=1)
    local_counts = jnp.sum(picked, axis=0)
    kept_mask = slot_rank < capacity
    slot_total = experts * capacity
    slot_index = jnp.where(kept_mask, flat_routes * capacity + slot_rank, slot_total)
    token_index = jnp.arange(tok_rows * top_count, dtype=jnp.int32) // top_count
    source = jnp.zeros((slot_total + 1,), jnp.int32).at[slot_index].set(token_index)[:slot_total]
    filled = jnp.zeros((slot_total + 1,), jnp.bool_).at[slot_index].set(True)[:slot_total]
    send_rows = jnp.where(filled[:, None], tokens[source], jnp.zeros((), jnp.bfloat16))
    send_rows = send_rows.reshape(groups, per_device, capacity, feature_width)
    gathered = [lax.all_gather(w, "dp", axis=1, tiled=True) for w in (w_gate, w_up, w_down)]
    produced = expert_products(
        lax.all_to_all(send_rows, "expert", split_axis=0, concat_axis=0, tiled=True), *gathered
    ).astype(jnp.bfloat16)
    returned = lax.all_to_all(produced, "expert", split_axis=0, concat_axis=0, tiled=True)
    flat_out = returned.reshape(slot_total, feature_width)
    fetched = flat_out[jnp.minimum(slot_index, slot_total - 1)]
    entry_weight = jnp.where(kept_mask, route_weight.reshape(-1), jnp.float32(0.0))
    weighted = fetched.astype(jnp.float32) * entry_weight[:, None]
    mixed = jnp.sum(weighted.reshape(tok_rows, top_count, feature_width), axis=1).astype(
        jnp.bfloat16
    )
    mean_load = tok_rows * top_count * lax.axis_size("dp") * groups
    totals = lax.psum(local_counts.astype(jnp.float32), ("dp", "expert"))
    new_bias = bias + bias_rate * jnp.sign(mean_load - experts * totals)
    return (mixed, new_bias, totals.astype(jnp.int32))


def layer_kernel(
    zs, capacity, per_device,
    tokens, routes_t, weights_t, w_gate, w_up, w_down,
    out, totals,
    tok, table, gate_w, up_w, down_own, down_far, hidden,
    part1, keep1, recv1, part2, keep2, recv2, part3, keep3, recv3, tally, tally_in,
    tok_in, tok_out, tab_in, tab_out, own_sem, w_in, w_out, d_in, d_out,
    s1_in, s1_out, s2_in, s2_out, s3_in, s3_out, t_in, t_out,
):
    rows, width = tokens.shape
    top = routes_t.shape[0]
    experts = table.shape[1] // 2
    ff = w_gate.shape[0]
    unit = ff // per_device
    cd = width // chunks
    slots = tok.shape[0]
    dp, ex = lax.axis_index("dp"), lax.axis_index("expert")
    y, x = dp // 2, dp % 2
    z, c = ex // 2, ex % 2

    def at(y_, x_, z_, c_):
        return (y_ * 2 + x_, z_ * 2 + c_)

    def slot(y_, z_, c_):
        return (y_ * zs + z_) * 2 + c_

    def far(step):
        return lax.rem(z + step, zs)

    mate = at(y, x, z, 1 - c)
    y_side = at(1 - y, x, z, c)
    x_side = at(y, 1 - x, z, c)
    me = slot(y, z, c)

    barrier = pltpu.get_barrier_semaphore()
    partners = [mate, y_side, x_side] + [at(y, x, far(s), c) for s in range(1, zs)]
    for partner in partners:
        pl.semaphore_signal(barrier, inc=1, device_id=partner, device_id_type=MESH)

    own = [
        pltpu.make_async_copy(tokens, tok.at[me], own_sem.at[0]),
        pltpu.make_async_copy(w_gate, gate_w.at[0], own_sem.at[1]),
        pltpu.make_async_copy(w_up, up_w.at[0], own_sem.at[2]),
        pltpu.make_async_copy(w_down, down_own, own_sem.at[3]),
    ]
    for copy in own:
        copy.start()

    labels = lax.broadcasted_iota(jnp.int32, (experts, rows), 0)
    picked = jnp.zeros((experts, rows), jnp.float32)
    weight = jnp.zeros((experts, rows), jnp.float32)
    for k in range(top):
        same = labels == routes_t[k : k + 1, :]
        picked += jnp.where(same, 1.0, 0.0)
        weight += jnp.where(same, weights_t[k : k + 1, :], 0.0)
    earlier = jnp.where(
        lax.broadcasted_iota(jnp.int32, (rows, rows), 0)
        < lax.broadcasted_iota(jnp.int32, (rows, rows), 1),
        1.0,
        0.0,
    )
    rank = jnp.dot(
        picked.astype(jnp.bfloat16),
        earlier.astype(jnp.bfloat16),
        preferred_element_type=jnp.float32,
    )
    table[me, 0:experts, :] = jnp.where(rank < capacity, weight, 0.0)
    table[me, experts : 2 * experts, :] = picked

    pl.semaphore_wait(barrier, len(partners))

    sent = []

    def remote(src, dst, ssem, rsem, device, keep=True):
        copy = pltpu.make_async_remote_copy(
            src_ref=src, dst_ref=dst, send_sem=ssem, recv_sem=rsem,
            device_id=device, device_id_type=MESH,
        )
        copy.start()
        if keep:
            sent.append(copy)

    def landed(ref, sem):
        pltpu.make_async_copy(ref, ref, sem).wait()

    def pass_on(n, index, device, source=None):
        remote(table.at[index], table.at[index], tab_out.at[n], tab_in.at[index], device, False)
        remote(
            tok.at[index] if source is None else source, tok.at[index],
            tok_out.at[n], tok_in.at[index], device, False,
        )

    def passed(n):
        pltpu.make_async_copy(table.at[0], table.at[0], tab_out.at[n]).wait()
        pltpu.make_async_copy(tok.at[0], tok.at[0], tok_out.at[n]).wait()

    def arrived(index):
        landed(table.at[index], tab_in.at[index])
        landed(tok.at[index], tok_in.at[index])

    above, below = z < zs - 1, z > 0
    z_up, z_down = at(y, x, z + 1, c), at(y, x, z - 1, c)

    for j in range(per_device):
        units = pl.ds(j * unit, unit)
        remote(w_gate.at[units], gate_w.at[1, units], w_out.at[0, j], w_in.at[0, j], x_side)
        remote(w_up.at[units], up_w.at[1, units], w_out.at[1, j], w_in.at[1, j], x_side)
    @pl.when(above)
    def _():
        pass_on(z, me, z_up, tokens)

    @pl.when(below)
    def _():
        pass_on(zs + z, me, z_down, tokens)

    pass_on(2 * zs + z, me, y_side, tokens)
    pass_on(3 * zs + me // 2, me, mate, tokens)
    for j in range(chunks):
        remote(
            w_down.at[:, j * cd : (j + 1) * cd], down_far.at[j], d_out.at[j], d_in.at[j], x_side
        )
    for copy in own:
        copy.wait()

    def column(index, j):
        row = table[index, pl.ds(ex * per_device + j, 1), :]
        return jnp.transpose(jnp.broadcast_to(row, (rows, rows)))

    def scales(index):
        columns = [column(index, j) for j in range(per_device)]
        lanes = columns[0].shape[1]
        place = lax.broadcasted_iota(jnp.int32, (rows, lanes), 1)
        pieces = []
        for t in range(ff // lanes):
            piece = columns[0]
            for j in range(1, per_device):
                piece = jnp.where(place + t * lanes >= j * unit, columns[j], piece)
            pieces.append(piece)
        return jnp.concatenate(pieces, axis=1)

    nt = (((1,), (1,)), ((), ()))

    def act(block, gate_t, up_t):
        gate = lax.dot_general(block, gate_t, nt, preferred_element_type=jnp.float32)
        up = lax.dot_general(block, up_t, nt, preferred_element_type=jnp.float32)
        return gate / (1.0 + jnp.exp(-gate)) * up

    batch = 4

    def relay(source, onward, device, n):
        index = slot(y, source, c)
        arrived(index)

        @pl.when(onward)
        def _():
            pass_on(n + source, index, device)

        pass_on(2 * zs + source, index, y_side)
        pass_on(3 * zs + index // 2, index, mate)

    for d in range(1, zs):

        @pl.when(z >= d)
        def _():
            relay(z - d, above, z_up, 0)

        @pl.when(z + d < zs)
        def _():
            relay(z + d, below, z_down, zs)

    def from_y(source):
        index = slot(1 - y, source, c)
        arrived(index)
        pass_on(3 * zs + index // 2, index, mate)

    from_y(z)
    for d in range(1, zs):

        @pl.when(z >= d)
        def _():
            from_y(z - d)

        @pl.when(z + d < zs)
        def _():
            from_y(z + d)

    def from_mate(i, carry):
        arrived(2 * i + 1 - c)
        return carry

    lax.fori_loop(0, slots // 2, from_mate, 0)

    def own_half(q, carry):
        first = q * batch
        block = tok[pl.ds(first, batch)].reshape(batch * rows, width)
        value = act(block, gate_w[0], up_w[0])
        for i in range(batch):
            scaled = value[i * rows : (i + 1) * rows] * scales(first + i)
            hidden[first + i, :, 0:ff] = scaled.astype(jnp.bfloat16)
        return carry

    lax.fori_loop(0, slots // batch, own_half, 0)

    def add_tally(i, total):
        return total + table[i, experts : 2 * experts, :]

    tally[...] = lax.fori_loop(0, slots, add_tally, jnp.zeros((experts, rows), jnp.float32))

    remote(tally, tally_in, t_out, t_in, x_side)

    for j in range(per_device):
        units = pl.ds(j * unit, unit)
        landed(gate_w.at[1, units], w_in.at[0, j])
        landed(up_w.at[1, units], w_in.at[1, j])

        def other_half(q, carry, j=j):
            first = q * batch
            block = tok[pl.ds(first, batch)].reshape(batch * rows, width)
            value = act(block, gate_w[1, j * unit : (j + 1) * unit], up_w[1, j * unit : (j + 1) * unit])
            for i in range(batch):
                scaled = value[i * rows : (i + 1) * rows] * column(first + i, j)[:, 0:1]
                hidden[first + i, :, ff + j * unit : ff + (j + 1) * unit] = scaled.astype(
                    jnp.bfloat16
                )
            return carry

        if j < per_device - 1:
            lax.fori_loop(0, slots // batch, other_half, 0)

    groups = slots // batch // 2
    starts = ((1 - y) * groups, y * groups)

    def down(j, part):
        def step(q, carry):
            near = hidden[pl.ds(q * batch, batch)].reshape(batch * rows, 2 * ff)
            value = jnp.dot(
                near[:, :ff], down_own[:, j * cd : (j + 1) * cd],
                preferred_element_type=jnp.float32,
            ) + jnp.dot(near[:, ff:], down_far[j], preferred_element_type=jnp.float32)
            for i in range(batch // 2):
                one = value[2 * i * rows : (2 * i + 1) * rows]
                two = value[(2 * i + 1) * rows : (2 * i + 2) * rows]
                keep1[j, q * (batch // 2) + i] = jnp.where(c == 0, one, two)
                part1[j, q * (batch // 2) + i] = jnp.where(c == 0, two, one).astype(jnp.bfloat16)
            return carry

        lax.fori_loop(starts[part], starts[part] + groups, step, 0)
        held = pl.ds(starts[part] * (batch // 2), zs)
        remote(
            part1.at[j, held], recv1.at[j, held], s1_out.at[j, part], s1_in.at[j, part], mate
        )

    def over_core(j):
        landed(recv1.at[j, pl.ds((1 - y) * zs, zs)], s1_in.at[j, 0])

        def away(i, carry):
            n = (1 - y) * zs + i
            value = keep1[j, n] + recv1[j, n].astype(jnp.float32)
            part2[j, i] = value.astype(jnp.bfloat16)
            return carry

        lax.fori_loop(0, zs, away, 0)
        remote(part2.at[j], recv2.at[j], s2_out.at[j], s2_in.at[j], y_side)

        landed(recv1.at[j, pl.ds(y * zs, zs)], s1_in.at[j, 1])

        def home(i, carry):
            n = y * zs + i
            keep2[j, i] = keep1[j, n] + recv1[j, n].astype(jnp.float32)
            return carry

        lax.fori_loop(0, zs, home, 0)

    def over_y(j):
        landed(recv2.at[j], s2_in.at[j])

        for s in range(1, zs):
            n = far(s)
            value = keep2[j, n] + recv2[j, n].astype(jnp.float32)
            part3[j, s - 1] = value.astype(jnp.bfloat16)
            remote(
                part3.at[j, s - 1], recv3.at[j, s - 1],
                s3_out.at[j, s - 1], s3_in.at[j, s - 1], at(y, x, n, c),
            )
        keep3[j] = keep2[j, z] + recv2[j, z].astype(jnp.float32)

    def over_z(j):
        value = keep3[j]
        for s in range(1, zs):
            landed(recv3.at[j, s - 1], s3_in.at[j, s - 1])
            value += recv3[j, s - 1].astype(jnp.float32)
        out[:, j * cd : (j + 1) * cd] = value.astype(jnp.bfloat16)

    for j in range(chunks + 3):
        if j < chunks:
            if j > 0:
                landed(down_far.at[j], d_in.at[j])
            for part in range(2):
                if j == 0:
                    lax.fori_loop(starts[part], starts[part] + groups, other_half, 0)
                    if part == 0:
                        landed(down_far.at[0], d_in.at[0])
                down(j, part)
        if 0 <= j - 1 < chunks:
            over_core(j - 1)
        if 0 <= j - 2 < chunks:
            over_y(j - 2)
        if 0 <= j - 3 < chunks:
            over_z(j - 3)

    landed(tally_in, t_in)
    count = jnp.sum(tally[...] + tally_in[...], axis=1, keepdims=True)
    totals[...] = jnp.broadcast_to(count, totals.shape)
    for copy in sent:
        copy.wait_send()

    def z_sent(source, carry):
        @pl.when(jnp.logical_and(above, source <= z))
        def _():
            passed(source)

        @pl.when(jnp.logical_and(below, source >= z))
        def _():
            passed(zs + source)

        passed(2 * zs + source)
        return carry

    lax.fori_loop(0, zs, z_sent, 0)

    def mate_sent(i, carry):
        passed(3 * zs + i)
        return carry

    lax.fori_loop(0, slots // 2, mate_sent, 0)


def group_scratch(zs, rows, width, ff, experts):
    slots = 4 * zs
    cd = width // chunks
    bf, f32 = jnp.bfloat16, jnp.float32
    return [
        ((slots, rows, width), bf),
        ((slots, 2 * experts, rows), f32),
        ((2, ff, width), bf),
        ((2, ff, width), bf),
        ((ff, width), bf),
        ((chunks, ff, cd), bf),
        ((slots, rows, 2 * ff), bf),
        ((chunks, slots // 2, rows, cd), bf),
        ((chunks, slots // 2, rows, cd), f32),
        ((chunks, slots // 2, rows, cd), bf),
        ((chunks, zs, rows, cd), bf),
        ((chunks, zs, rows, cd), f32),
        ((chunks, zs, rows, cd), bf),
        ((chunks, zs - 1, rows, cd), bf),
        ((chunks, rows, cd), f32),
        ((chunks, zs - 1, rows, cd), bf),
        ((experts, rows), f32),
        ((experts, rows), f32),
    ]


def group_body(zs, tokens, routes, route_weight, bias, w_gate, w_up, w_down):
    rows, width = tokens.shape
    experts = bias.shape[0]
    per_device, unit, _ = w_gate.shape
    ff = per_device * unit
    top = routes.shape[1]
    capacity = 5 * rows * top // (4 * experts)
    slots = 4 * zs
    dma = pltpu.SemaphoreType.DMA
    vmem = pl.BlockSpec(memory_space=pltpu.VMEM)
    anywhere = pl.BlockSpec(memory_space=pl.ANY)
    mixed, totals = pl.pallas_call(
        functools.partial(layer_kernel, zs, capacity, per_device),
        out_shape=(
            jax.ShapeDtypeStruct((rows, width), jnp.bfloat16),
            jax.ShapeDtypeStruct((experts, rows), jnp.float32),
        ),
        in_specs=[anywhere, vmem, vmem, anywhere, anywhere, anywhere],
        out_specs=(vmem, vmem),
        scratch_shapes=[
            pltpu.VMEM(shape, kind)
            for shape, kind in group_scratch(zs, rows, width, ff, experts)
        ]
        + [
            dma((slots,)), dma((5 * zs,)), dma((slots,)), dma((5 * zs,)), dma((4,)),
            dma((2, per_device)), dma((2, per_device)), dma((chunks,)), dma((chunks,)),
            dma((chunks, 2)), dma((chunks, 2)), dma((chunks,)), dma((chunks,)),
            dma((chunks, zs - 1)), dma((chunks, zs - 1)), dma, dma,
        ],
        compiler_params=pltpu.CompilerParams(
            collective_id=0, has_side_effects=True, vmem_limit_bytes=VMEM_BYTES
        ),
    )(
        tokens, routes.T, route_weight.T,
        w_gate.reshape(ff, width), w_up.reshape(ff, width), w_down.reshape(ff, width),
    )
    counts = totals[:, 0]
    mean_load = rows * top * lax.axis_size("dp") * lax.axis_size("expert")
    new_bias = bias + bias_rate * jnp.sign(mean_load - experts * counts)
    return (mixed, new_bias, counts.astype(jnp.int32))


def body(tokens, routes, route_weight, bias, w_gate, w_up, w_down):
    rows, width = tokens.shape
    per_device, unit, _ = w_gate.shape
    groups = lax.axis_size("expert")
    zs = groups // 2
    held = group_scratch(zs, rows, width, per_device * unit, bias.shape[0])
    total = 0
    for shape, kind in held:
        size = jnp.dtype(kind).itemsize
        for extent in shape:
            size *= extent
        total += size
    args = (tokens, routes, route_weight, bias, w_gate, w_up, w_down)
    if lax.axis_size("dp") == 4 and groups % 2 == 0 and zs % 2 == 0 and total < 0.85 * VMEM_BYTES:
        return group_body(zs, *args)
    return exchange_body(*args)


def solution(mesh):
    placed = (
        P(("dp", "expert"), None),
        P(("dp", "expert"), None),
        P(("dp", "expert"), None),
        P(),
        P("expert", "dp", None),
        P("expert", "dp", None),
        P("expert", "dp", None),
    )
    return jax.shard_map(
        body,
        mesh=mesh,
        in_specs=placed,
        out_specs=(P(("dp", "expert"), None), P(), P()),
        check_vma=False,
    )
```

profile of v0, /device:TPU:0, one launch (start us, length us, event | category | flops | bytes accessed | tf_op | source)
XLA Modules:
  0.0 145.6 jit_solution(8196577129015364851)
XLA Ops:
  0.6 139.8 %shard_map.94 = (bf16[128,2048]{1,0:T(8,128)(2,1)}, f32[16,128]{1,0:T(8,128)}) custom-call(bf16[128,2048]{1,0:T(8,128)(2,1)} %tokens.1, s32[8,128]{1,0:T(8,128)} %bitcast.8, f32[8,128]{1,0:T(8,128)} %bitcast.9, bf16[384,2048]{1,0:T(8,128)(2,1)} %bitcast.5, bf16[384,2048]{1,0:T(8,128)(2,1)} %bitcast.6, bf16[384,2048]{1,0:T(8,128)(2,1)} %bitcast.7), custom_call_target="tpu_custom_call" | custom-call | tf_op jit(solution)/shard_map/pallas_call | solution.py:436
  140.4 0.8 multiply_reduce_fusion
  141.2 1.2 add.3
  142.4 1.3 convert_reduce_fusion
  143.7 1.9 %copy.11 = bf16[128,2048]{1,0:T(8,128)(2,1)} copy(bf16[128,2048]{1,0:T(8,128)(2,1)} %get-tuple-element.10) | data formatting | bytes 1048576
where the time goes:
time: 146 us
  Pallas kernels  140 us (96%)
  other arithmetic  3.31 us (2%)
  local copies, waits for them, and re-layouts  1.88 us (1%)
    pallas_call x1, Pallas kernels, group_body(): pl.pallas_call(functools.partial(layer_kernel, zs, capacity, per_device),...  140 us

commit v1 on v0

v1 whole, which is shorter than its diff:
```python
import functools

import jax
import jax.numpy as jnp
from jax import lax
from jax.experimental import pallas as pl
from jax.experimental.pallas import tpu as pltpu
from jax.sharding import PartitionSpec as P

bias_rate = 0.05
MESH = pl.DeviceIdType.MESH
VMEM_BYTES = 67043328
chunks = 16
lane_count = 128


def expert_products(received, gate_w, up_w, down_w):
    gate_act = jnp.einsum("sjcd,jfd->sjcf", received, gate_w, preferred_element_type=jnp.float32)
    up_act = jnp.einsum("sjcd,jfd->sjcf", received, up_w, preferred_element_type=jnp.float32)
    hidden = (jax.nn.silu(gate_act) * up_act).astype(jnp.bfloat16)
    return jnp.einsum("sjcf,jfd->sjcd", hidden, down_w, preferred_element_type=jnp.float32)


def exchange_body(tokens, routes, route_weight, bias, w_gate, w_up, w_down):
    tok_rows, feature_width = tokens.shape
    top_count = routes.shape[1]
    experts = bias.shape[0]
    groups = lax.axis_size("expert")
    per_device = w_gate.shape[0]
    capacity = 5 * tok_rows * top_count // (4 * experts)
    flat_routes = routes.reshape(-1)
    labels = jnp.arange(experts, dtype=jnp.int32)
    picked = (flat_routes[:, None] == labels[None, :]).astype(jnp.int32)
    running = jnp.cumsum(picked, axis=0) - picked
    slot_rank = jnp.sum(running * picked, axis=1)
    local_counts = jnp.sum(picked, axis=0)
    kept_mask = slot_rank < capacity
    slot_total = experts * capacity
    slot_index = jnp.where(kept_mask, flat_routes * capacity + slot_rank, slot_total)
    token_index = jnp.arange(tok_rows * top_count, dtype=jnp.int32) // top_count
    source = jnp.zeros((slot_total + 1,), jnp.int32).at[slot_index].set(token_index)[:slot_total]
    filled = jnp.zeros((slot_total + 1,), jnp.bool_).at[slot_index].set(True)[:slot_total]
    send_rows = jnp.where(filled[:, None], tokens[source], jnp.zeros((), jnp.bfloat16))
    send_rows = send_rows.reshape(groups, per_device, capacity, feature_width)
    gathered = [lax.all_gather(w, "dp", axis=1, tiled=True) for w in (w_gate, w_up, w_down)]
    produced = expert_products(
        lax.all_to_all(send_rows, "expert", split_axis=0, concat_axis=0, tiled=True), *gathered
    ).astype(jnp.bfloat16)
    returned = lax.all_to_all(produced, "expert", split_axis=0, concat_axis=0, tiled=True)
    flat_out = returned.reshape(slot_total, feature_width)
    fetched = flat_out[jnp.minimum(slot_index, slot_total - 1)]
    entry_weight = jnp.where(kept_mask, route_weight.reshape(-1), jnp.float32(0.0))
    weighted = fetched.astype(jnp.float32) * entry_weight[:, None]
    mixed = jnp.sum(weighted.reshape(tok_rows, top_count, feature_width), axis=1).astype(
        jnp.bfloat16
    )
    mean_load = tok_rows * top_count * lax.axis_size("dp") * groups
    totals = lax.psum(local_counts.astype(jnp.float32), ("dp", "expert"))
    new_bias = bias + bias_rate * jnp.sign(mean_load - experts * totals)
    return (mixed, new_bias, totals.astype(jnp.int32))


def layer_kernel(
    zs, capacity, per_device,
    tokens, routes_t, weights_t, w_gate, w_up, w_down,
    out, totals,
    tok, table, gate_w, up_w, down_w, scale, hidden, held,
    part1, keep1, recv1, part2, keep2, recv2, tally, tally_in,
    own_sem, own_d, tok_in, tok_out, tab_in, tab_out, w_in, w_out, d_in, d_out,
    m_in, m_out, md_in, md_out, f_in, f_out, fd_in, fd_out,
    s1_in, s1_out, s2_in, s2_out, t_in, t_out,
):
    rows, width = tokens.shape
    top = routes_t.shape[0]
    experts = table.shape[1] // 2
    pieces, lanes, _ = w_gate.shape
    ff = pieces * lanes
    unit = ff // per_device
    cd = width // chunks
    slots = tok.shape[0]
    dp, ex = lax.axis_index("dp"), lax.axis_index("expert")
    y, x = dp // 2, dp % 2
    z, c = ex // 2, ex % 2

    def at(y_, x_, z_, c_):
        return (y_ * 2 + x_, z_ * 2 + c_)

    def slot(y_, z_):
        return y_ * zs + z_

    def far(step):
        return lax.rem(z + step, zs)

    mate = at(y, x, z, 1 - c)
    y_side = at(1 - y, x, z, c)
    x_side = at(y, 1 - x, z, c)
    x_mate = at(y, 1 - x, z, 1 - c)
    me = slot(y, z)

    barrier = pltpu.get_barrier_semaphore()
    partners = [mate, y_side, x_side, x_mate] + [at(y, x, far(s), c) for s in range(1, zs)]
    for partner in partners:
        pl.semaphore_signal(barrier, inc=1, device_id=partner, device_id_type=MESH)

    def span(j):
        return pl.ds(pl.multiple_of(j * cd, cd), cd)

    own = [
        pltpu.make_async_copy(tokens, tok.at[me], own_sem.at[0]),
        pltpu.make_async_copy(w_gate, gate_w.at[0, :, 0], own_sem.at[1]),
        pltpu.make_async_copy(w_up, up_w.at[0, :, 0], own_sem.at[2]),
    ]
    for copy in own:
        copy.start()

    def own_down(j):
        return pltpu.make_async_copy(w_down.at[:, :, span(j)], down_w.at[j, 0, :, 0], own_d.at[j])

    labels = lax.broadcasted_iota(jnp.int32, (experts, rows), 0)
    picked = jnp.zeros((experts, rows), jnp.float32)
    weight = jnp.zeros((experts, rows), jnp.float32)
    for k in range(top):
        same = labels == routes_t[k : k + 1, :]
        picked += jnp.where(same, 1.0, 0.0)
        weight += jnp.where(same, weights_t[k : k + 1, :], 0.0)
    earlier = jnp.where(
        lax.broadcasted_iota(jnp.int32, (rows, rows), 0)
        < lax.broadcasted_iota(jnp.int32, (rows, rows), 1),
        1.0,
        0.0,
    )
    rank = jnp.dot(
        picked.astype(jnp.bfloat16),
        earlier.astype(jnp.bfloat16),
        preferred_element_type=jnp.float32,
    )
    table[me, 0:experts, :] = jnp.where(rank < capacity, weight, 0.0)
    table[me, experts : 2 * experts, :] = picked

    pl.semaphore_wait(barrier, len(partners))

    sent = []

    def remote(src, dst, ssem, rsem, device, keep=True):
        copy = pltpu.make_async_remote_copy(
            src_ref=src, dst_ref=dst, send_sem=ssem, recv_sem=rsem,
            device_id=device, device_id_type=MESH,
        )
        copy.start()
        if keep:
            sent.append(copy)

    def landed(ref, sem):
        pltpu.make_async_copy(ref, ref, sem).wait()

    def cross(n, p, source, target):
        remote(source.at[p], target.at[1, p, 0], w_out.at[n, p], w_in.at[n, p], x_side)

    def cross_down(j):
        remote(
            w_down.at[:, :, span(j)], down_w.at[j, 1, :, 0], d_out.at[j], d_in.at[j], x_side, False
        )

    for p in range(pieces):
        cross(0, p, w_gate, gate_w)
        if p == pieces - 1:
            cross_down(0)
        cross(1, p, w_up, up_w)

    def pass_on(n, index, device, source=None):
        remote(table.at[index], table.at[index], tab_out.at[n], tab_in.at[index], device, False)
        remote(
            tok.at[index] if source is None else source, tok.at[index],
            tok_out.at[n], tok_in.at[index], device, False,
        )

    def passed(n):
        pltpu.make_async_copy(table.at[0], table.at[0], tab_out.at[n]).wait()
        pltpu.make_async_copy(tok.at[0], tok.at[0], tok_out.at[n]).wait()

    def arrived(index):
        landed(table.at[index], tab_in.at[index])
        landed(tok.at[index], tok_in.at[index])

    above, below = z < zs - 1, z > 0
    z_up, z_down = at(y, x, z + 1, c), at(y, x, z - 1, c)

    @pl.when(above)
    def _():
        pass_on(z, me, z_up, tokens)

    @pl.when(below)
    def _():
        pass_on(zs + z, me, z_down, tokens)

    pass_on(2 * zs + z, me, y_side, tokens)

    remote(w_gate, gate_w.at[0, :, 1], m_out.at[0], m_in.at[0], mate)
    remote(w_up, up_w.at[0, :, 1], m_out.at[1], m_in.at[1], mate)

    def spread(j, carry):
        @pl.when(j > 0)
        def _():
            cross_down(j)

        own_down(j).start()
        remote(
            w_down.at[:, :, span(j)], down_w.at[j, 0, :, 1], md_out.at[j], md_in.at[j], mate, False
        )
        return carry

    lax.fori_loop(0, chunks, spread, 0)

    for copy in own:
        copy.wait()

    def relay(source, onward, device, n):
        index = slot(y, source)
        arrived(index)

        @pl.when(onward)
        def _():
            pass_on(n + source, index, device)

        pass_on(2 * zs + source, index, y_side)

    for d in range(1, zs):

        @pl.when(z >= d)
        def _():
            relay(z - d, above, z_up, 0)

        @pl.when(z + d < zs)
        def _():
            relay(z + d, below, z_down, zs)

    def forward(n, p, target):
        landed(target.at[1, p, 0], w_in.at[n, p])
        remote(target.at[1, p, 0], target.at[1, p, 1], f_out.at[n, p], f_in.at[n, p], mate)

    for p in range(pieces - 1):
        forward(0, p, gate_w)
        forward(1, p, up_w)

    def from_y(i, carry):
        arrived(slot(1 - y, i))
        return carry

    lax.fori_loop(0, zs, from_y, 0)

    def add_tally(i, total):
        return total + table[i, experts : 2 * experts, :]

    tally[...] = lax.fori_loop(0, slots, add_tally, jnp.zeros((experts, rows), jnp.float32))
    for i, device in enumerate((x_side, mate, x_mate)):
        remote(tally, tally_in.at[i], t_out.at[i], t_in.at[i], device)

    place = lax.broadcasted_iota(jnp.int32, (rows, lanes), 1)

    def fill(index, carry):
        for k in range(2):
            first = (z * 2 + (c if k == 0 else 1 - c)) * per_device
            columns = []
            for j in range(per_device):
                row = table[index, pl.ds(first + j, 1), :]
                columns.append(jnp.transpose(jnp.broadcast_to(row, (lanes, rows))))
            for p in range(pieces):
                piece = columns[0]
                for j in range(1, per_device):
                    piece = jnp.where(place + p * lanes >= j * unit, columns[j], piece)
                scale[p, index, :, k * lanes : (k + 1) * lanes] = piece
        return carry

    lax.fori_loop(0, slots, fill, 0)

    nt = (((1,), (1,)), ((), ()))
    pair = 2 * lanes

    def project(q, h, p, source):
        block = tok[pl.ds(q * zs, zs)].reshape(zs * rows, width)
        return lax.dot_general(
            block, source[h, p].reshape(pair, width), nt, preferred_element_type=jnp.float32
        )

    def activate(q, h, p, gate, up):
        value = gate / (1.0 + jnp.exp(-gate)) * up
        first = (h * pieces + p) * pair
        for i in range(zs):
            scaled = value[i * rows : (i + 1) * rows] * scale[p, q * zs + i]
            hidden[q * zs + i, :, first : first + pair] = scaled.astype(jnp.bfloat16)

    def both(h, p):
        def step(q, carry):
            activate(q, h, p, project(q, h, p, gate_w), project(q, h, p, up_w))
            return carry

        lax.fori_loop(0, 2, step, 0)

    landed(gate_w.at[0, :, 1], m_in.at[0])
    landed(up_w.at[0, :, 1], m_in.at[1])
    for p in range(pieces):
        both(0, p)
    for p in range(pieces - 1):
        landed(gate_w.at[1, p, 1], f_in.at[0, p])
        landed(up_w.at[1, p, 1], f_in.at[1, p])
        both(1, p)

    last = pieces - 1
    forward(0, last, gate_w)
    landed(gate_w.at[1, last, 1], f_in.at[0, last])

    def hold(q, carry):
        held[q] = project(q, 1, last, gate_w)
        return carry

    lax.fori_loop(0, 2, hold, 0)

    def fetch(j):
        landed(down_w.at[j, 1, :, 0], d_in.at[j])
        remote(
            down_w.at[j, 1, :, 0], down_w.at[j, 1, :, 1], fd_out.at[j], fd_in.at[j], mate, False
        )

    def ready(j):
        own_down(j).wait()
        landed(down_w.at[j, 0, :, 1], md_in.at[j])
        landed(down_w.at[j, 1, :, 1], fd_in.at[j])

    fetch(0)
    forward(1, last, up_w)
    ready(0)
    landed(up_w.at[1, last, 1], f_in.at[1, last])

    def finish(q):
        activate(q, 1, last, held[q], project(q, 1, last, up_w))

    def down(q, j):
        near = hidden[pl.ds(q * zs, zs)].reshape(zs * rows, 4 * ff)
        return jnp.dot(
            near, down_w[j].reshape(4 * ff, cd), preferred_element_type=jnp.float32
        ).reshape(zs, rows, cd)

    def away(j):
        part1[j] = down(1 - y, j).astype(jnp.bfloat16)
        remote(part1.at[j], recv1.at[j], s1_out.at[j], s1_in.at[j], y_side, False)

    def home(j):
        keep1[j] = down(y, j)

    def over_y(j):
        landed(recv1.at[j], s1_in.at[j])
        for s in range(1, zs):
            n = far(s)
            value = keep1[j, n] + recv1[j, n].astype(jnp.float32)
            part2[j, s - 1] = value.astype(jnp.bfloat16)
            remote(
                part2.at[j, s - 1], recv2.at[j, s - 1],
                s2_out.at[j, s - 1], s2_in.at[j, s - 1], at(y, x, n, c), False,
            )
        keep2[j] = keep1[j, z] + recv1[j, z].astype(jnp.float32)

    def over_z(j):
        value = keep2[j]
        for s in range(1, zs):
            landed(recv2.at[j, s - 1], s2_in.at[j, s - 1])
            value += recv2[j, s - 1].astype(jnp.float32)
        out[:, span(j)] = value.astype(jnp.bfloat16)

    finish(1 - y)
    away(0)
    finish(y)
    home(0)

    lag_y, lag_z = 2, 4

    def step(j, carry):
        fetch(j)
        ready(j)
        away(j)
        home(j)

        @pl.when(j >= lag_y)
        def _():
            over_y(j - lag_y)

        @pl.when(j >= lag_z)
        def _():
            over_z(j - lag_z)

        return carry

    lax.fori_loop(1, chunks, step, 0)

    def drain(j, carry):
        @pl.when(j < chunks + lag_y)
        def _():
            over_y(j - lag_y)

        over_z(j - lag_z)
        return carry

    lax.fori_loop(chunks, chunks + lag_z, drain, 0)

    count = tally[...]
    for i in range(3):
        landed(tally_in.at[i], t_in.at[i])
        count += tally_in[i]
    totals[...] = count
    for copy in sent:
        copy.wait_send()

    def gone(j, carry):
        @pl.when(j > 0)
        def _():
            landed(down_w.at[j, 1, :, 0], d_out.at[j])

        landed(down_w.at[j, 1, :, 0], md_out.at[j])
        landed(down_w.at[j, 1, :, 0], fd_out.at[j])
        landed(part1.at[j], s1_out.at[j])
        for s in range(1, zs):
            landed(part2.at[j, s - 1], s2_out.at[j, s - 1])
        return carry

    landed(down_w.at[0, 1, :, 0], d_out.at[0])
    lax.fori_loop(0, chunks, gone, 0)

    def z_sent(source, carry):
        @pl.when(jnp.logical_and(above, source <= z))
        def _():
            passed(source)

        @pl.when(jnp.logical_and(below, source >= z))
        def _():
            passed(zs + source)

        passed(2 * zs + source)
        return carry

    lax.fori_loop(0, zs, z_sent, 0)


def group_scratch(zs, rows, width, ff, experts):
    slots = 2 * zs
    cd = width // chunks
    pieces = ff // lane_count
    bf, f32 = jnp.bfloat16, jnp.float32
    return [
        ((slots, rows, width), bf),
        ((slots, 2 * experts, rows), f32),
        ((2, pieces, 2, lane_count, width), bf),
        ((2, pieces, 2, lane_count, width), bf),
        ((chunks, 2, pieces, 2, lane_count, cd), bf),
        ((pieces, slots, rows, 2 * lane_count), f32),
        ((slots, rows, 4 * ff), bf),
        ((2, zs * rows, 2 * lane_count), f32),
        ((chunks, zs, rows, cd), bf),
        ((chunks, zs, rows, cd), f32),
        ((chunks, zs, rows, cd), bf),
        ((chunks, zs - 1, rows, cd), bf),
        ((chunks, rows, cd), f32),
        ((chunks, zs - 1, rows, cd), bf),
        ((experts, rows), f32),
        ((3, experts, rows), f32),
    ]


def finish_kernel(load, mixed, tally, bias, out, new_bias, counts):
    out[...] = mixed[...]
    experts, rows = tally.shape
    row = lax.dot_general(
        jnp.ones((8, rows), jnp.bfloat16), tally[...].astype(jnp.bfloat16),
        (((1,), (1,)), ((), ())), preferred_element_type=jnp.float32,
    )[0:1]
    spare = load - experts * row
    step = jnp.where(spare > 0.0, bias_rate, jnp.where(spare < 0.0, -bias_rate, 0.0))
    new_bias[...] = bias[...] + step
    counts[...] = row.astype(jnp.int32)


def group_body(zs, tokens, routes, route_weight, bias, w_gate, w_up, w_down):
    rows, width = tokens.shape
    experts = bias.shape[0]
    per_device, unit, _ = w_gate.shape
    ff = per_device * unit
    top = routes.shape[1]
    capacity = 5 * rows * top // (4 * experts)
    slots = 2 * zs
    pieces = ff // lane_count
    dma = pltpu.SemaphoreType.DMA
    vmem = pl.BlockSpec(memory_space=pltpu.VMEM)
    anywhere = pl.BlockSpec(memory_space=pl.ANY)
    split = (pieces, lane_count, width)
    mixed, totals = pl.pallas_call(
        functools.partial(layer_kernel, zs, capacity, per_device),
        out_shape=(
            jax.ShapeDtypeStruct((rows, width), jnp.bfloat16),
            jax.ShapeDtypeStruct((experts, rows), jnp.float32),
        ),
        in_specs=[anywhere, vmem, vmem, anywhere, anywhere, anywhere],
        out_specs=(vmem, vmem),
        scratch_shapes=[
            pltpu.VMEM(shape, kind)
            for shape, kind in group_scratch(zs, rows, width, ff, experts)
        ]
        + [
            dma((3,)), dma((chunks,)),
            dma((slots,)), dma((3 * zs,)), dma((slots,)), dma((3 * zs,)),
            dma((2, pieces)), dma((2, pieces)), dma((chunks,)), dma((chunks,)),
            dma((2,)), dma((2,)), dma((chunks,)), dma((chunks,)),
            dma((2, pieces)), dma((2, pieces)), dma((chunks,)), dma((chunks,)),
            dma((chunks,)), dma((chunks,)), dma((chunks, zs - 1)), dma((chunks, zs - 1)),
            dma((3,)), dma((3,)),
        ],
        compiler_params=pltpu.CompilerParams(
            collective_id=0, has_side_effects=True, vmem_limit_bytes=VMEM_BYTES
        ),
    )(
        tokens, routes.T, route_weight.T,
        w_gate.reshape(split), w_up.reshape(split), w_down.reshape(split),
    )
    mean_load = rows * top * lax.axis_size("dp") * lax.axis_size("expert")
    mixed, new_bias, counts = pl.pallas_call(
        functools.partial(finish_kernel, mean_load),
        out_shape=(
            jax.ShapeDtypeStruct((rows, width), jnp.bfloat16),
            jax.ShapeDtypeStruct((1, experts), jnp.float32),
            jax.ShapeDtypeStruct((1, experts), jnp.int32),
        ),
        in_specs=[vmem, vmem, vmem],
        out_specs=(vmem, vmem, vmem),
    )(mixed, totals, bias.reshape(1, experts))
    return (mixed, new_bias.reshape(experts), counts.reshape(experts))


def body(tokens, routes, route_weight, bias, w_gate, w_up, w_down):
    rows, width = tokens.shape
    per_device, unit, _ = w_gate.shape
    ff = per_device * unit
    groups = lax.axis_size("expert")
    zs = groups // 2
    held = group_scratch(zs, rows, width, ff, bias.shape[0])
    total = 0
    for shape, kind in held:
        size = jnp.dtype(kind).itemsize
        for extent in shape:
            size *= extent
        total += size
    args = (tokens, routes, route_weight, bias, w_gate, w_up, w_down)
    fits = total < 0.85 * VMEM_BYTES and rows == lane_count
    even = ff % lane_count == 0 and width % (chunks * lane_count) == 0
    if lax.axis_size("dp") == 4 and groups % 2 == 0 and zs % 2 == 0 and fits and even:
        return group_body(zs, *args)
    return exchange_body(*args)


def solution(mesh):
    placed = (
        P(("dp", "expert"), None),
        P(("dp", "expert"), None),
        P(("dp", "expert"), None),
        P(),
        P("expert", "dp", None),
        P("expert", "dp", None),
        P("expert", "dp", None),
    )
    return jax.shard_map(
        body,
        mesh=mesh,
        in_specs=placed,
        out_specs=(P(("dp", "expert"), None), P(), P()),
        check_vma=False,
    )
```

time: 146 us -> 144 us (0.986)
  other arithmetic: 3.31 us -> 0 us
  Pallas kernels: 140 us -> 143 us
  local copies, waits for them, and re-layouts: 1.88 us -> 0 us
    pallas_call x0 -> x1, Pallas kernels: none -> 1.89 us  [group_body(): pl.pallas_call(functools.partial(finish_kernel, mean_load), out_shape=(ja...]
    unnamed x1 -> x0, local copies, waits for them, and re-layouts: 1.88 us -> none
    pallas_call x1, Pallas kernels: 140 us -> 141 us  [group_body(): pl.pallas_call(functools.partial(layer_kernel, zs, capacity, per_device),...]
where the time goes in v1:
time: 144 us
  Pallas kernels  143 us (99%)
    pallas_call x1, Pallas kernels, group_body(): pl.pallas_call(functools.partial(layer_kernel, zs, capacity, per_device),...  141 us

profile of v1, /device:TPU:0, one launch (start us, length us, event | category | flops | bytes accessed | tf_op | source)
XLA Modules:
  0.0 143.9 jit_solution(14569522664451134469)
XLA Ops:
  0.6 141.3 %shard_map.94 = (bf16[128,2048]{1,0:T(8,128)(2,1)}, f32[16,128]{1,0:T(8,128)}) custom-call(bf16[128,2048]{1,0:T(8,128)(2,1)} %tokens.1, s32[8,128]{1,0:T(8,128)} %bitcast.11, f32[8,128]{1,0:T(8,128)} %bitcast.12, bf16[3,128,2048]{2,1,0:T(8,128)(2,1)} %bitcast.8, bf16[3,128,2048]{2,1,0:T(8,128)(2,1)} %bitcast.9, bf16[3,128,2048]{2,1,0:T(8,128)(2,1)} %bitcast.10), custom_call_target="tpu_custom_call" | custom-call | tf_op jit(solution)/shard_map/pallas_call | solution.py:493
  142.0 1.9 %shard_map.95 = (bf16[128,2048]{1,0:T(8,128)(2,1)}, f32[1,16]{1,0:T(1,128)}, s32[1,16]{1,0:T(1,128)}) custom-call(bf16[128,2048]{1,0:T(8,128)(2,1)} %get-tuple-element.8.mixed, f32[16,128]{1,0:T(8,128)} %get-tuple-element.9.tally, f32[1,16]{1,0:T(1,128)} %bitcast.13), custom_call_target="tpu_custom_call" | custom-call | tf_op jit(solution)/shard_map/pallas_call | solution.py:522

commit v2 on v1

--- a/solution.py
+++ b/solution.py
@@ -12,6 +12,8 @@
 VMEM_BYTES = 67043328
 chunks = 16
 lane_count = 128
+crossed = (4, 8)
+straight_chunks = 2
 
 
 def expert_products(received, gate_w, up_w, down_w):
@@ -65,10 +67,12 @@
     tokens, routes_t, weights_t, w_gate, w_up, w_down,
     out, totals,
     tok, table, gate_w, up_w, down_w, scale, hidden, held,
-    part1, keep1, recv1, part2, keep2, recv2, tally, tally_in,
+    part1, keep1, recv1, part2, keep2, recv2, far2, mix2,
+    keep3, part3, recv3, far3, own3, mix3, part4, recv4, early, tally, tally_in,
     own_sem, own_d, tok_in, tok_out, tab_in, tab_out, w_in, w_out, d_in, d_out,
     m_in, m_out, md_in, md_out, f_in, f_out, fd_in, fd_out,
-    s1_in, s1_out, s2_in, s2_out, t_in, t_out,
+    s1_in, s1_out, s2_in, s2_out, c2_in, s3_in, s3_out, c3_in, s4_in, s4_out,
+    t_in, t_out, turn,
 ):
     rows, width = tokens.shape
     top = routes_t.shape[0]
@@ -114,7 +118,7 @@
         copy.start()
 
     def own_down(j):
-        return pltpu.make_async_copy(w_down.at[:, :, span(j)], down_w.at[j, 0, :, 0], own_d.at[j])
+        return pltpu.make_async_copy(w_down.at[:, :, span(j)], down_w.at[j, 0, :, 0], own_d)
 
     labels = lax.broadcasted_iota(jnp.int32, (experts, rows), 0)
     picked = jnp.zeros((experts, rows), jnp.float32)
@@ -139,44 +143,45 @@
 
     pl.semaphore_wait(barrier, len(partners))
 
-    sent = []
-
-    def remote(src, dst, ssem, rsem, device, keep=True):
+    def remote(src, dst, ssem, rsem, device):
         copy = pltpu.make_async_remote_copy(
             src_ref=src, dst_ref=dst, send_sem=ssem, recv_sem=rsem,
             device_id=device, device_id_type=MESH,
         )
         copy.start()
-        if keep:
-            sent.append(copy)
+        return copy
 
     def landed(ref, sem):
         pltpu.make_async_copy(ref, ref, sem).wait()
 
     def cross(n, p, source, target):
-        remote(source.at[p], target.at[1, p, 0], w_out.at[n, p], w_in.at[n, p], x_side)
+        final = n == 1 and p == pieces - 1
+        return remote(
+            source.at[p], target.at[1, p, 0], w_out.at[1 if final else 0], w_in.at[n, p],
+            x_side,
+        )
 
     def cross_down(j):
         remote(
-            w_down.at[:, :, span(j)], down_w.at[j, 1, :, 0], d_out.at[j], d_in.at[j], x_side, False
+            w_down.at[:, :, span(j)], down_w.at[j, 1, :, 0], d_out, d_in.at[j], x_side
         )
 
     for p in range(pieces):
         cross(0, p, w_gate, gate_w)
         if p == pieces - 1:
             cross_down(0)
-        cross(1, p, w_up, up_w)
+        last_up = cross(1, p, w_up, up_w)
 
     def pass_on(n, index, device, source=None):
-        remote(table.at[index], table.at[index], tab_out.at[n], tab_in.at[index], device, False)
+        remote(table.at[index], table.at[index], tab_out.at[n], tab_in.at[index], device)
         remote(
             tok.at[index] if source is None else source, tok.at[index],
-            tok_out.at[n], tok_in.at[index], device, False,
+            tok_out.at[n], tok_in.at[index], device,
         )
 
-    def passed(n):
-        pltpu.make_async_copy(table.at[0], table.at[0], tab_out.at[n]).wait()
-        pltpu.make_async_copy(tok.at[0], tok.at[0], tok_out.at[n]).wait()
+    def passed(n, count):
+        landed(table.at[pl.ds(0, count)], tab_out.at[n])
+        landed(tok.at[pl.ds(0, count)], tok_out.at[n])
 
     def arrived(index):
         landed(table.at[index], tab_in.at[index])
@@ -187,25 +192,21 @@
 
     @pl.when(above)
     def _():
-        pass_on(z, me, z_up, tokens)
+        pass_on(0, me, z_up, tokens)
 
     @pl.when(below)
     def _():
-        pass_on(zs + z, me, z_down, tokens)
-
-    pass_on(2 * zs + z, me, y_side, tokens)
-
-    remote(w_gate, gate_w.at[0, :, 1], m_out.at[0], m_in.at[0], mate)
-    remote(w_up, up_w.at[0, :, 1], m_out.at[1], m_in.at[1], mate)
+        pass_on(0, me, z_down, tokens)
+
+    pass_on(1, me, y_side, tokens)
+
+    remote(w_gate, gate_w.at[0, :, 1], m_out, m_in.at[0], mate)
+    remote(w_up, up_w.at[0, :, 1], m_out, m_in.at[1], mate)
 
     def spread(j, carry):
-        @pl.when(j > 0)
-        def _():
-            cross_down(j)
-
         own_down(j).start()
         remote(
-            w_down.at[:, :, span(j)], down_w.at[j, 0, :, 1], md_out.at[j], md_in.at[j], mate, False
+            w_down.at[:, :, span(j)], down_w.at[j, 0, :, 1], md_out, md_in, mate
         )
         return carry
 
@@ -214,29 +215,29 @@
     for copy in own:
         copy.wait()
 
-    def relay(source, onward, device, n):
+    def relay(source, onward, device):
         index = slot(y, source)
         arrived(index)
 
         @pl.when(onward)
         def _():
-            pass_on(n + source, index, device)
-
-        pass_on(2 * zs + source, index, y_side)
+            pass_on(0, index, device)
+
+        pass_on(1, index, y_side)
 
     for d in range(1, zs):
 
         @pl.when(z >= d)
         def _():
-            relay(z - d, above, z_up, 0)
+            relay(z - d, above, z_up)
 
         @pl.when(z + d < zs)
         def _():
-            relay(z + d, below, z_down, zs)
+            relay(z + d, below, z_down)
 
     def forward(n, p, target):
         landed(target.at[1, p, 0], w_in.at[n, p])
-        remote(target.at[1, p, 0], target.at[1, p, 1], f_out.at[n, p], f_in.at[n, p], mate)
+        remote(target.at[1, p, 0], target.at[1, p, 1], f_out, f_in.at[n, p], mate)
 
     for p in range(pieces - 1):
         forward(0, p, gate_w)
@@ -253,7 +254,7 @@
 
     tally[...] = lax.fori_loop(0, slots, add_tally, jnp.zeros((experts, rows), jnp.float32))
     for i, device in enumerate((x_side, mate, x_mate)):
-        remote(tally, tally_in.at[i], t_out.at[i], t_in.at[i], device)
+        remote(tally, tally_in.at[i], t_out, t_in.at[i], device)
 
     place = lax.broadcasted_iota(jnp.int32, (rows, lanes), 1)
 
@@ -282,16 +283,20 @@
             block, source[h, p].reshape(pair, width), nt, preferred_element_type=jnp.float32
         )
 
+    def gated(q, p, gate):
+        value = gate / (1.0 + jnp.exp(-gate))
+        factor = scale[p, pl.ds(q * zs, zs)].reshape(zs * rows, pair)
+        return value * factor
+
     def activate(q, h, p, gate, up):
-        value = gate / (1.0 + jnp.exp(-gate)) * up
         first = (h * pieces + p) * pair
-        for i in range(zs):
-            scaled = value[i * rows : (i + 1) * rows] * scale[p, q * zs + i]
-            hidden[q * zs + i, :, first : first + pair] = scaled.astype(jnp.bfloat16)
+        value = (gate * up).astype(jnp.bfloat16)
+        hidden[pl.ds(q * zs, zs), :, first : first + pair] = value.reshape(zs, rows, pair)
 
     def both(h, p):
         def step(q, carry):
-            activate(q, h, p, project(q, h, p, gate_w), project(q, h, p, up_w))
+            gate = gated(q, p, project(q, h, p, gate_w))
+            activate(q, h, p, gate, project(q, h, p, up_w))
             return carry
 
         lax.fori_loop(0, 2, step, 0)
@@ -310,7 +315,7 @@
     landed(gate_w.at[1, last, 1], f_in.at[0, last])
 
     def hold(q, carry):
-        held[q] = project(q, 1, last, gate_w)
+        held[q] = gated(q, last, project(q, 1, last, gate_w))
         return carry
 
     lax.fori_loop(0, 2, hold, 0)
@@ -318,21 +323,50 @@
     def fetch(j):
         landed(down_w.at[j, 1, :, 0], d_in.at[j])
         remote(
-            down_w.at[j, 1, :, 0], down_w.at[j, 1, :, 1], fd_out.at[j], fd_in.at[j], mate, False
+            down_w.at[j, 1, :, 0], down_w.at[j, 1, :, 1], fd_out, fd_in.at[j], mate
         )
 
     def ready(j):
-        own_down(j).wait()
-        landed(down_w.at[j, 0, :, 1], md_in.at[j])
         landed(down_w.at[j, 1, :, 1], fd_in.at[j])
 
     fetch(0)
+    landed(down_w.at[:, 0, :, 0], own_d)
+    landed(down_w.at[:, 0, :, 1], md_in)
+    ready(0)
+    known = 4 * ff - pair
+
+    def begin(q, carry):
+        near = hidden[pl.ds(q * zs, zs), :, 0:known].reshape(zs * rows, known)
+        weights = down_w[0].reshape(4 * ff, cd)[0:known]
+        early[q] = jnp.dot(near, weights, preferred_element_type=jnp.float32)
+        return carry
+
+    lax.fori_loop(0, 2, begin, 0)
+
+    last_up.wait_send()
+    pl.semaphore_signal(turn, inc=1, device_id=mate, device_id_type=MESH)
+    pl.semaphore_wait(turn, 1)
+
+    def follow(j, carry):
+        cross_down(j)
+        return carry
+
+    lax.fori_loop(1, chunks, follow, 0)
     forward(1, last, up_w)
-    ready(0)
     landed(up_w.at[1, last, 1], f_in.at[1, last])
 
     def finish(q):
-        activate(q, 1, last, held[q], project(q, 1, last, up_w))
+        block = tok[pl.ds(q * zs, zs)].reshape(zs * rows, width)
+        part = up_w[1, last].reshape(pair, width)
+        half = width // 2
+        ups = [
+            lax.dot_general(
+                block[:, k * half : (k + 1) * half], part[:, k * half : (k + 1) * half],
+                nt, preferred_element_type=jnp.float32,
+            )
+            for k in range(2)
+        ]
+        activate(q, 1, last, held[q], ups[0] + ups[1])
 
     def down(q, j):
         near = hidden[pl.ds(q * zs, zs)].reshape(zs * rows, 4 * ff)
@@ -340,109 +374,227 @@
             near, down_w[j].reshape(4 * ff, cd), preferred_element_type=jnp.float32
         ).reshape(zs, rows, cd)
 
-    def away(j):
-        part1[j] = down(1 - y, j).astype(jnp.bfloat16)
-        remote(part1.at[j], recv1.at[j], s1_out.at[j], s1_in.at[j], y_side, False)
-
-    def home(j):
-        keep1[j] = down(y, j)
+    def down_first(q):
+        near = hidden[pl.ds(q * zs, zs), :, known : 4 * ff].reshape(zs * rows, pair)
+        weights = down_w[0].reshape(4 * ff, cd)[known : 4 * ff]
+        value = early[q] + jnp.dot(near, weights, preferred_element_type=jnp.float32)
+        return value.reshape(zs, rows, cd)
+
+    def away(j, value):
+        part1[j] = value.astype(jnp.bfloat16)
+        remote(part1.at[j], recv1.at[j], s1_out, s1_in.at[j], y_side)
+
+    end = jnp.logical_or(z == 0, z == zs - 1)
+    inner = jnp.logical_not(end)
+    beside = z + 1 - 2 * lax.rem(z, 2)
+    across = lax.rem(z + 2, zs)
+    mirror = zs - 1 - z
+    straight = jnp.where(end, across, mirror)
+    lane = jnp.where(end, 1, 2)
+
+    def out_z(j, value, part, recv, kept, mix, outs, ins, mix_in, direct=None):
+        def send(i, n, target, sem, device):
+            part[j, i] = value(n).astype(jnp.bfloat16)
+            remote(part.at[j, i], target, outs, sem, at(y, x, device, c))
+
+        send(0, beside, recv.at[j, 0], ins.at[j], beside)
+        send(1, straight, recv.at[j, lane], ins.at[j], straight)
+
+        def relayed():
+            @pl.when(end)
+            def _():
+                send(2, mirror, mix.at[j], mix_in.at[j], beside)
+
+            @pl.when(inner)
+            def _():
+                kept[j] = value(across)
+
+        def unrelayed():
+            @pl.when(end)
+            def _():
+                send(2, mirror, recv.at[j, 2], ins.at[j], mirror)
+
+            @pl.when(inner)
+            def _():
+                send(2, across, recv.at[j, 1], ins.at[j], across)
+
+        if direct is None:
+            relayed()
+        else:
+            pl.when(direct)(unrelayed)
+            pl.when(jnp.logical_not(direct))(relayed)
+
+    def merge(j, part, recv, kept, mix, outs, ins, mix_in):
+        @pl.when(inner)
+        def _():
+            landed(mix.at[j], mix_in.at[j])
+            part[j, 2] = (kept[j] + mix[j].astype(jnp.float32)).astype(jnp.bfloat16)
+            remote(
+                part.at[j, 2], recv.at[j, 1], outs, ins.at[j],
+                at(y, x, across, c),
+            )
+
+    def in_z(j, total, recv, ins, third):
+        def add(count):
+            landed(recv.at[j, pl.ds(0, count)], ins.at[j])
+            value = total[j]
+            for i in range(count):
+                value = value + recv[j, i].astype(jnp.float32)
+            total[j] = value
+
+        pl.when(third)(lambda: add(3))
+        pl.when(jnp.logical_not(third))(lambda: add(2))
+
+    def is_last(j):
+        return j >= chunks - straight_chunks
 
     def over_y(j):
         landed(recv1.at[j], s1_in.at[j])
-        for s in range(1, zs):
-            n = far(s)
-            value = keep1[j, n] + recv1[j, n].astype(jnp.float32)
-            part2[j, s - 1] = value.astype(jnp.bfloat16)
-            remote(
-                part2.at[j, s - 1], recv2.at[j, s - 1],
-                s2_out.at[j, s - 1], s2_in.at[j, s - 1], at(y, x, n, c), False,
-            )
-        keep2[j] = keep1[j, z] + recv1[j, z].astype(jnp.float32)
+
+        def value(n):
+            return keep1[j, n] + recv1[j, n].astype(jnp.float32)
+
+        out_z(j, value, part2, recv2, far2, mix2, s2_out, s2_in, c2_in, is_last(j))
+        keep2[j] = value(z)
+
+    def merge_y(j):
+        merge(j, part2, recv2, far2, mix2, s2_out, s2_in, c2_in)
 
     def over_z(j):
-        value = keep2[j]
-        for s in range(1, zs):
-            landed(recv2.at[j, s - 1], s2_in.at[j, s - 1])
-            value += recv2[j, s - 1].astype(jnp.float32)
+        in_z(j, keep2, recv2, s2_in, jnp.logical_or(inner, is_last(j)))
+        out[:, span(j)] = keep2[j].astype(jnp.bfloat16)
+
+    def first_z(b):
+        def value(n):
+            return keep3[b, :, n]
+
+        out_z(b, value, part3, recv3, far3, mix3, s3_out, s3_in, c3_in)
+        own3[b] = value(z)
+
+    def then_y(b):
+        in_z(b, own3, recv3, s3_in, inner)
+        part4[b] = own3[b, 1 - y].astype(jnp.bfloat16)
+        remote(part4.at[b], recv4.at[b], s4_out, s4_in.at[b], y_side)
+
+    def crossed_out(b, j):
+        landed(recv4.at[b], s4_in.at[b])
+        value = own3[b, y] + recv4[b].astype(jnp.float32)
         out[:, span(j)] = value.astype(jnp.bfloat16)
 
     finish(1 - y)
-    away(0)
+    away(0, down_first(1 - y))
+    fetch(1)
     finish(y)
-    home(0)
-
-    lag_y, lag_z = 2, 4
+    keep1[0] = down_first(y)
+
+    lag_y, lag_m, lag_z = 2, 6, 10
+    late = chunks - straight_chunks - 3
+
+    def plain(j):
+        ok = jnp.logical_and(j >= 0, j < chunks)
+        for special in crossed:
+            ok = jnp.logical_and(ok, j != special)
+        return ok
 
     def step(j, carry):
-        fetch(j)
-        ready(j)
-        away(j)
-        home(j)
-
-        @pl.when(j >= lag_y)
+        @pl.when(j < chunks)
+        def _():
+            ready(j)
+
+            @pl.when(plain(j))
+            def _():
+                away(j, down(1 - y, j))
+
+            for b, special in enumerate(crossed):
+
+                @pl.when(j == special)
+                def _(b=b):
+                    keep3[b, 1 - y] = down(1 - y, j)
+
+            @pl.when(j < chunks - 1)
+            def _():
+                fetch(j + 1)
+
+            @pl.when(plain(j))
+            def _():
+                keep1[j] = down(y, j)
+
+            for b, special in enumerate(crossed):
+
+                @pl.when(j == special)
+                def _(b=b):
+                    keep3[b, y] = down(y, j)
+                    first_z(b)
+
+        for lag, first, past in (
+            (lag_m, 0, late), (lag_m - 2, late, chunks - straight_chunks)
+        ):
+            due = jnp.logical_and(j - lag >= first, j - lag < past)
+
+            @pl.when(jnp.logical_and(plain(j - lag), due))
+            def _(lag=lag):
+                merge_y(j - lag)
+
+        @pl.when(plain(j - lag_y))
         def _():
             over_y(j - lag_y)
 
-        @pl.when(j >= lag_z)
+        for b, special in enumerate(crossed):
+
+            @pl.when(j == special + 5)
+            def _(b=b):
+                merge(b, part3, recv3, far3, mix3, s3_out, s3_in, c3_in)
+
+            @pl.when(j == special + 7)
+            def _(b=b):
+                then_y(b)
+
+            @pl.when(j == special + 11)
+            def _(b=b, special=special):
+                crossed_out(b, special)
+
+        @pl.when(plain(j - lag_z))
         def _():
             over_z(j - lag_z)
 
         return carry
 
-    lax.fori_loop(1, chunks, step, 0)
-
-    def drain(j, carry):
-        @pl.when(j < chunks + lag_y)
-        def _():
-            over_y(j - lag_y)
-
-        over_z(j - lag_z)
-        return carry
-
-    lax.fori_loop(chunks, chunks + lag_z, drain, 0)
+    lax.fori_loop(1, chunks + lag_z, step, 0)
 
     count = tally[...]
     for i in range(3):
         landed(tally_in.at[i], t_in.at[i])
         count += tally_in[i]
     totals[...] = count
-    for copy in sent:
-        copy.wait_send()
-
-    def gone(j, carry):
-        @pl.when(j > 0)
-        def _():
-            landed(down_w.at[j, 1, :, 0], d_out.at[j])
-
-        landed(down_w.at[j, 1, :, 0], md_out.at[j])
-        landed(down_w.at[j, 1, :, 0], fd_out.at[j])
-        landed(part1.at[j], s1_out.at[j])
-        for s in range(1, zs):
-            landed(part2.at[j, s - 1], s2_out.at[j, s - 1])
-        return carry
-
-    landed(down_w.at[0, 1, :, 0], d_out.at[0])
-    lax.fori_loop(0, chunks, gone, 0)
-
-    def z_sent(source, carry):
-        @pl.when(jnp.logical_and(above, source <= z))
-        def _():
-            passed(source)
-
-        @pl.when(jnp.logical_and(below, source >= z))
-        def _():
-            passed(zs + source)
-
-        passed(2 * zs + source)
-        return carry
-
-    lax.fori_loop(0, zs, z_sent, 0)
+    landed(gate_w.at[:, :, 1], m_out)
+    landed(gate_w.at[:, :, 1], f_out)
+    landed(tok.at[pl.ds(0, 2 * pieces - 1)], w_out.at[0])
+    landed(tally_in, t_out)
+
+    for sem in (d_out, md_out, fd_out):
+        landed(down_w.at[:, 1, :, 0], sem)
+    usual = pl.ds(0, chunks - len(crossed))
+    landed(part1.at[usual], s1_out)
+    landed(part2.at[usual], s2_out)
+    landed(part3, s3_out)
+    landed(part4, s4_out)
+
+    passed(1, zs)
+
+    @pl.when(end)
+    def _():
+        passed(0, 1)
+
+    @pl.when(inner)
+    def _():
+        passed(0, zs + 1)
 
 
 def group_scratch(zs, rows, width, ff, experts):
     slots = 2 * zs
     cd = width // chunks
     pieces = ff // lane_count
+    twice = len(crossed)
     bf, f32 = jnp.bfloat16, jnp.float32
     return [
         ((slots, rows, width), bf),
@@ -459,13 +611,25 @@
         ((chunks, zs - 1, rows, cd), bf),
         ((chunks, rows, cd), f32),
         ((chunks, zs - 1, rows, cd), bf),
+        ((chunks, rows, cd), f32),
+        ((chunks, rows, cd), bf),
+        ((twice, 2, zs, rows, cd), f32),
+        ((twice, zs - 1, 2, rows, cd), bf),
+        ((twice, zs - 1, 2, rows, cd), bf),
+        ((twice, 2, rows, cd), f32),
+        ((twice, 2, rows, cd), f32),
+        ((twice, 2, rows, cd), bf),
+        ((twice, rows, cd), bf),
+        ((twice, rows, cd), bf),
+        ((2, zs * rows, cd), f32),
         ((experts, rows), f32),
         ((3, experts, rows), f32),
     ]
 
 
-def finish_kernel(load, mixed, tally, bias, out, new_bias, counts):
-    out[...] = mixed[...]
+def finish_kernel(load, mixed, tally, bias, out, new_bias, counts, done):
+    copy = pltpu.make_async_copy(mixed, out, done)
+    copy.start()
     experts, rows = tally.shape
     row = lax.dot_general(
         jnp.ones((8, rows), jnp.bfloat16), tally[...].astype(jnp.bfloat16),
@@ -475,6 +639,7 @@
     step = jnp.where(spare > 0.0, bias_rate, jnp.where(spare < 0.0, -bias_rate, 0.0))
     new_bias[...] = bias[...] + step
     counts[...] = row.astype(jnp.int32)
+    copy.wait()
 
 
 def group_body(zs, tokens, routes, route_weight, bias, w_gate, w_up, w_down):
@@ -486,6 +651,7 @@
     capacity = 5 * rows * top // (4 * experts)
     slots = 2 * zs
     pieces = ff // lane_count
+    twice = len(crossed)
     dma = pltpu.SemaphoreType.DMA
     vmem = pl.BlockSpec(memory_space=pltpu.VMEM)
     anywhere = pl.BlockSpec(memory_space=pl.ANY)
@@ -493,8 +659,8 @@
     mixed, totals = pl.pallas_call(
         functools.partial(layer_kernel, zs, capacity, per_device),
         out_shape=(
-            jax.ShapeDtypeStruct((rows, width), jnp.bfloat16),
-            jax.ShapeDtypeStruct((experts, rows), jnp.float32),
+            pltpu.VMEM((rows, width), jnp.bfloat16),
+            pltpu.VMEM((experts, rows), jnp.float32),
         ),
         in_specs=[anywhere, vmem, vmem, anywhere, anywhere, anywhere],
         out_specs=(vmem, vmem),
@@ -503,21 +669,22 @@
             for shape, kind in group_scratch(zs, rows, width, ff, experts)
         ]
         + [
-            dma((3,)), dma((chunks,)),
-            dma((slots,)), dma((3 * zs,)), dma((slots,)), dma((3 * zs,)),
-            dma((2, pieces)), dma((2, pieces)), dma((chunks,)), dma((chunks,)),
-            dma((2,)), dma((2,)), dma((chunks,)), dma((chunks,)),
-            dma((2, pieces)), dma((2, pieces)), dma((chunks,)), dma((chunks,)),
-            dma((chunks,)), dma((chunks,)), dma((chunks, zs - 1)), dma((chunks, zs - 1)),
-            dma((3,)), dma((3,)),
+            dma((3,)), dma, dma((slots,)), dma((2,)), dma((slots,)), dma((2,)),
+            dma((2, pieces)), dma((2,)), dma((chunks,)), dma, dma((2,)), dma, dma, dma,
+            dma((2, pieces)), dma, dma((chunks,)), dma,
+            dma((chunks,)), dma, dma((chunks,)), dma,
+            dma((chunks,)), dma((twice,)), dma, dma((twice,)),
+            dma((twice,)), dma, dma((3,)), dma, pltpu.SemaphoreType.REGULAR,
         ],
         compiler_params=pltpu.CompilerParams(
-            collective_id=0, has_side_effects=True, vmem_limit_bytes=VMEM_BYTES
+            collective_id=0, has_side_effects=True, vmem_limit_bytes=60000000
         ),
     )(
         tokens, routes.T, route_weight.T,
         w_gate.reshape(split), w_up.reshape(split), w_down.reshape(split),
     )
+    mixed = pltpu.with_memory_space_constraint(mixed, pltpu.VMEM)
+    totals = pltpu.with_memory_space_constraint(totals, pltpu.VMEM)
     mean_load = rows * top * lax.axis_size("dp") * lax.axis_size("expert")
     mixed, new_bias, counts = pl.pallas_call(
         functools.partial(finish_kernel, mean_load),
@@ -527,7 +694,8 @@
             jax.ShapeDtypeStruct((1, experts), jnp.int32),
         ),
         in_specs=[vmem, vmem, vmem],
-        out_specs=(vmem, vmem, vmem),
+        out_specs=(anywhere, vmem, vmem),
+        scratch_shapes=[dma],
     )(mixed, totals, bias.reshape(1, experts))
     return (mixed, new_bias.reshape(experts), counts.reshape(experts))
 
@@ -548,7 +716,7 @@
     args = (tokens, routes, route_weight, bias, w_gate, w_up, w_down)
     fits = total < 0.85 * VMEM_BYTES and rows == lane_count
     even = ff % lane_count == 0 and width % (chunks * lane_count) == 0
-    if lax.axis_size("dp") == 4 and groups % 2 == 0 and zs % 2 == 0 and fits and even:
+    if lax.axis_size("dp") == 4 and groups % 2 == 0 and zs == 4 and fits and even:
         return group_body(zs, *args)
     return exchange_body(*args)
 

time: 144 us -> 134 us (0.931)
  Pallas kernels: 143 us -> 133 us
    pallas_call x1, Pallas kernels: 141 us -> 131 us  [group_body(): pl.pallas_call(functools.partial(layer_kernel, zs, capacity, per_device),...]
where the time goes in v2:
time: 134 us; the launch traced here: 133 us
  Pallas kernels  133 us (99%)
    pallas_call x1, Pallas kernels, group_body(): pl.pallas_call(functools.partial(layer_kernel, zs, capacity, per_device),...  131 us

profile of v2, /device:TPU:0, one launch (start us, length us, event | category | flops | bytes accessed | tf_op | source)
XLA Modules:
  0.0 133.5 jit_solution(17818519517159901261)
XLA Ops:
  0.6 130.8 %shard_map.94 = (bf16[128,2048]{1,0:T(8,128)(2,1)S(1)}, f32[16,128]{1,0:T(8,128)S(1)}) custom-call(bf16[128,2048]{1,0:T(8,128)(2,1)} %tokens.1, s32[8,128]{1,0:T(8,128)} %bitcast.11, f32[8,128]{1,0:T(8,128)} %bitcast.12, bf16[3,128,2048]{2,1,0:T(8,128)(2,1)} %bitcast.8, bf16[3,128,2048]{2,1,0:T(8,128)(2,1)} %bitcast.9, bf16[3,128,2048]{2,1,0:T(8,128)(2,1)} %bitcast.10), custom_call_target="tpu_custom_call" | custom-call | tf_op jit(solution)/shard_map/pallas_call | solution.py:659
  131.5 2.0 %shard_map.95 = (bf16[128,2048]{1,0:T(8,128)(2,1)}, f32[1,16]{1,0:T(1,128)}, s32[1,16]{1,0:T(1,128)}) custom-call(bf16[128,2048]{1,0:T(8,128)(2,1)S(1)} %get-tuple-element.8.mixed, f32[16,128]{1,0:T(8,128)S(1)} %get-tuple-element.9.tally, f32[1,16]{1,0:T(1,128)} %bitcast.13), custom_call_target="tpu_custom_call" | custom-call | tf_op jit(solution)/shard_map/pallas_call | solution.py:689

commit v3 on v2

--- a/solution.py
+++ b/solution.py
@@ -12,8 +12,9 @@
 VMEM_BYTES = 67043328
 chunks = 16
 lane_count = 128
-crossed = (4, 8)
-straight_chunks = 2
+copies = 8
+crossed = (3, 6)
+straight_chunks = 1
 
 
 def expert_products(received, gate_w, up_w, down_w):
@@ -63,16 +64,16 @@
 
 
 def layer_kernel(
-    zs, capacity, per_device,
-    tokens, routes_t, weights_t, w_gate, w_up, w_down,
-    out, totals,
-    tok, table, gate_w, up_w, down_w, scale, hidden, held,
+    zs, capacity, per_device, load,
+    tokens, routes_any, weights_any, bias_any, w_gate, w_up, w_down,
+    out, new_bias, counts,
+    routes_t, weights_t, bias, tok, table, gate_w, up_w, down_w, scale, hidden, held,
     part1, keep1, recv1, part2, keep2, recv2, far2, mix2,
     keep3, part3, recv3, far3, own3, mix3, part4, recv4, early, tally, tally_in,
     own_sem, own_d, tok_in, tok_out, tab_in, tab_out, w_in, w_out, d_in, d_out,
     m_in, m_out, md_in, md_out, f_in, f_out, fd_in, fd_out,
     s1_in, s1_out, s2_in, s2_out, c2_in, s3_in, s3_out, c3_in, s4_in, s4_out,
-    t_in, t_out, turn,
+    s5_in, t_in, t_out, turn,
 ):
     rows, width = tokens.shape
     top = routes_t.shape[0]
@@ -113,12 +114,91 @@
         pltpu.make_async_copy(tokens, tok.at[me], own_sem.at[0]),
         pltpu.make_async_copy(w_gate, gate_w.at[0, :, 0], own_sem.at[1]),
         pltpu.make_async_copy(w_up, up_w.at[0, :, 0], own_sem.at[2]),
+        pltpu.make_async_copy(routes_any, routes_t, own_sem.at[3]),
+        pltpu.make_async_copy(weights_any, weights_t, own_sem.at[4]),
+        pltpu.make_async_copy(bias_any, bias, own_sem.at[5]),
     ]
     for copy in own:
         copy.start()
 
     def own_down(j):
         return pltpu.make_async_copy(w_down.at[:, :, span(j)], down_w.at[j, 0, :, 0], own_d)
+
+    pl.semaphore_wait(barrier, len(partners))
+
+    def remote(src, dst, ssem, rsem, device):
+        copy = pltpu.make_async_remote_copy(
+            src_ref=src, dst_ref=dst, send_sem=ssem, recv_sem=rsem,
+            device_id=device, device_id_type=MESH,
+        )
+        copy.start()
+        return copy
+
+    def landed(ref, sem):
+        pltpu.make_async_copy(ref, ref, sem).wait()
+
+    def cross(n, p, source, target):
+        final = n == 1 and p == pieces - 1
+        return remote(
+            source.at[p], target.at[1, p, 0], w_out.at[1 if final else 0], w_in.at[n, p],
+            x_side,
+        )
+
+    def cross_down(j):
+        remote(
+            w_down.at[:, :, span(j)], down_w.at[j, 1, :, 0], d_out, d_in.at[j], x_side
+        )
+
+    for p in range(pieces):
+        cross(0, p, w_gate, gate_w)
+        last_up = cross(1, p, w_up, up_w)
+    cross_down(0)
+
+    def pass_table(n, index, device):
+        remote(table.at[index], table.at[index], tab_out.at[n], tab_in.at[index], device)
+
+    def pass_tokens(n, index, device, source):
+        remote(source, tok.at[index], tok_out.at[n], tok_in.at[index], device)
+
+    def pass_on(n, index, device):
+        pass_table(n, index, device)
+        pass_tokens(n, index, device, tok.at[index])
+
+    def passed(n, count):
+        landed(table.at[pl.ds(0, count)], tab_out.at[n])
+        landed(tok.at[pl.ds(0, count)], tok_out.at[n])
+
+    def arrived(index):
+        landed(table.at[index], tab_in.at[index])
+        landed(tok.at[index], tok_in.at[index])
+
+    above, below = z < zs - 1, z > 0
+    z_up, z_down = at(y, x, z + 1, c), at(y, x, z - 1, c)
+
+    @pl.when(above)
+    def _():
+        pass_tokens(0, me, z_up, tokens)
+
+    @pl.when(below)
+    def _():
+        pass_tokens(0, me, z_down, tokens)
+
+    pass_tokens(1, me, y_side, tokens)
+
+    remote(w_gate, gate_w.at[0, :, 1], m_out, m_in.at[0], mate)
+    remote(w_up, up_w.at[0, :, 1], m_out, m_in.at[1], mate)
+
+    def spread(j, carry):
+        own_down(j).start()
+        remote(
+            w_down.at[:, :, span(j)], down_w.at[j, 0, :, 1], md_out, md_in, mate
+        )
+        return carry
+
+    lax.fori_loop(0, chunks, spread, 0)
+
+    for copy in own[3:]:
+        copy.wait()
 
     labels = lax.broadcasted_iota(jnp.int32, (experts, rows), 0)
     picked = jnp.zeros((experts, rows), jnp.float32)
@@ -141,78 +221,16 @@
     table[me, 0:experts, :] = jnp.where(rank < capacity, weight, 0.0)
     table[me, experts : 2 * experts, :] = picked
 
-    pl.semaphore_wait(barrier, len(partners))
-
-    def remote(src, dst, ssem, rsem, device):
-        copy = pltpu.make_async_remote_copy(
-            src_ref=src, dst_ref=dst, send_sem=ssem, recv_sem=rsem,
-            device_id=device, device_id_type=MESH,
-        )
-        copy.start()
-        return copy
-
-    def landed(ref, sem):
-        pltpu.make_async_copy(ref, ref, sem).wait()
-
-    def cross(n, p, source, target):
-        final = n == 1 and p == pieces - 1
-        return remote(
-            source.at[p], target.at[1, p, 0], w_out.at[1 if final else 0], w_in.at[n, p],
-            x_side,
-        )
-
-    def cross_down(j):
-        remote(
-            w_down.at[:, :, span(j)], down_w.at[j, 1, :, 0], d_out, d_in.at[j], x_side
-        )
-
-    for p in range(pieces):
-        cross(0, p, w_gate, gate_w)
-        if p == pieces - 1:
-            cross_down(0)
-        last_up = cross(1, p, w_up, up_w)
-
-    def pass_on(n, index, device, source=None):
-        remote(table.at[index], table.at[index], tab_out.at[n], tab_in.at[index], device)
-        remote(
-            tok.at[index] if source is None else source, tok.at[index],
-            tok_out.at[n], tok_in.at[index], device,
-        )
-
-    def passed(n, count):
-        landed(table.at[pl.ds(0, count)], tab_out.at[n])
-        landed(tok.at[pl.ds(0, count)], tok_out.at[n])
-
-    def arrived(index):
-        landed(table.at[index], tab_in.at[index])
-        landed(tok.at[index], tok_in.at[index])
-
-    above, below = z < zs - 1, z > 0
-    z_up, z_down = at(y, x, z + 1, c), at(y, x, z - 1, c)
-
     @pl.when(above)
     def _():
-        pass_on(0, me, z_up, tokens)
+        pass_table(0, me, z_up)
 
     @pl.when(below)
     def _():
-        pass_on(0, me, z_down, tokens)
-
-    pass_on(1, me, y_side, tokens)
-
-    remote(w_gate, gate_w.at[0, :, 1], m_out, m_in.at[0], mate)
-    remote(w_up, up_w.at[0, :, 1], m_out, m_in.at[1], mate)
-
-    def spread(j, carry):
-        own_down(j).start()
-        remote(
-            w_down.at[:, :, span(j)], down_w.at[j, 0, :, 1], md_out, md_in, mate
-        )
-        return carry
-
-    lax.fori_loop(0, chunks, spread, 0)
-
-    for copy in own:
+        pass_table(0, me, z_down)
+
+    pass_table(1, me, y_side)
+    for copy in own[:3]:
         copy.wait()
 
     def relay(source, onward, device):
@@ -329,15 +347,13 @@
     def ready(j):
         landed(down_w.at[j, 1, :, 1], fd_in.at[j])
 
-    fetch(0)
     landed(down_w.at[:, 0, :, 0], own_d)
     landed(down_w.at[:, 0, :, 1], md_in)
-    ready(0)
-    known = 4 * ff - pair
+    known = 2 * ff
 
     def begin(q, carry):
         near = hidden[pl.ds(q * zs, zs), :, 0:known].reshape(zs * rows, known)
-        weights = down_w[0].reshape(4 * ff, cd)[0:known]
+        weights = down_w[0, 0].reshape(known, cd)
         early[q] = jnp.dot(near, weights, preferred_element_type=jnp.float32)
         return carry
 
@@ -366,7 +382,9 @@
             )
             for k in range(2)
         ]
-        activate(q, 1, last, held[q], ups[0] + ups[1])
+        first = (2 * pieces - 1) * pair
+        value = (held[q] * ups[0] + held[q] * ups[1]).astype(jnp.bfloat16)
+        hidden[pl.ds(q * zs, zs), :, first : first + pair] = value.reshape(zs, rows, pair)
 
     def down(q, j):
         near = hidden[pl.ds(q * zs, zs)].reshape(zs * rows, 4 * ff)
@@ -375,14 +393,10 @@
         ).reshape(zs, rows, cd)
 
     def down_first(q):
-        near = hidden[pl.ds(q * zs, zs), :, known : 4 * ff].reshape(zs * rows, pair)
-        weights = down_w[0].reshape(4 * ff, cd)[known : 4 * ff]
+        near = hidden[pl.ds(q * zs, zs), :, known : 4 * ff].reshape(zs * rows, known)
+        weights = down_w[0, 1].reshape(known, cd)
         value = early[q] + jnp.dot(near, weights, preferred_element_type=jnp.float32)
         return value.reshape(zs, rows, cd)
-
-    def away(j, value):
-        part1[j] = value.astype(jnp.bfloat16)
-        remote(part1.at[j], recv1.at[j], s1_out, s1_in.at[j], y_side)
 
     end = jnp.logical_or(z == 0, z == zs - 1)
     inner = jnp.logical_not(end)
@@ -390,15 +404,28 @@
     across = lax.rem(z + 2, zs)
     mirror = zs - 1 - z
     straight = jnp.where(end, across, mirror)
+    longest = jnp.where(end, mirror, across)
+    order = (longest, straight, beside, z)
+    final = chunks - 1
+
+    def away(j, value):
+        part1[j] = value.astype(jnp.bfloat16)
+
+        @pl.when(j < final)
+        def _():
+            remote(part1.at[j], recv1.at[j], s1_out, s1_in.at[j], y_side)
+
+        @pl.when(j == final)
+        def _():
+            for i, n in enumerate(order):
+                remote(part1.at[j, n], recv1.at[j, n], s1_out, s5_in.at[i], y_side)
+
     lane = jnp.where(end, 1, 2)
 
     def out_z(j, value, part, recv, kept, mix, outs, ins, mix_in, direct=None):
         def send(i, n, target, sem, device):
             part[j, i] = value(n).astype(jnp.bfloat16)
             remote(part.at[j, i], target, outs, sem, at(y, x, device, c))
-
-        send(0, beside, recv.at[j, 0], ins.at[j], beside)
-        send(1, straight, recv.at[j, lane], ins.at[j], straight)
 
         def relayed():
             @pl.when(end)
@@ -423,6 +450,9 @@
         else:
             pl.when(direct)(unrelayed)
             pl.when(jnp.logical_not(direct))(relayed)
+
+        send(1, straight, recv.at[j, lane], ins.at[j], straight)
+        send(0, beside, recv.at[j, 0], ins.at[j], beside)
 
     def merge(j, part, recv, kept, mix, outs, ins, mix_in):
         @pl.when(inner)
@@ -448,6 +478,21 @@
     def is_last(j):
         return j >= chunks - straight_chunks
 
+    def last_y(j):
+        def value(n):
+            return keep1[j, n] + recv1[j, n].astype(jnp.float32)
+
+        targets = (jnp.where(end, 2, 1), lane, 0)
+        for i, n in enumerate(order):
+            landed(recv1.at[j, n], s5_in.at[i])
+            if i < zs - 1:
+                part2[j, i] = value(n).astype(jnp.bfloat16)
+                remote(
+                    part2.at[j, i], recv2.at[j, targets[i]], s2_out, s2_in.at[j],
+                    at(y, x, n, c),
+                )
+        keep2[j] = value(z)
+
     def over_y(j):
         landed(recv1.at[j], s1_in.at[j])
 
@@ -482,12 +527,28 @@
         out[:, span(j)] = value.astype(jnp.bfloat16)
 
     finish(1 - y)
+    fetch(0)
+    ready(0)
     away(0, down_first(1 - y))
+    finish(y)
     fetch(1)
-    finish(y)
     keep1[0] = down_first(y)
 
-    lag_y, lag_m, lag_z = 2, 6, 10
+    def tell():
+        count = tally[...]
+        for i in range(3):
+            landed(tally_in.at[i], t_in.at[i])
+            count += tally_in[i]
+        row = lax.dot_general(
+            jnp.ones((8, rows), jnp.bfloat16), count.astype(jnp.bfloat16), nt,
+            preferred_element_type=jnp.float32,
+        )[0:1]
+        spare = load - experts * row
+        change = jnp.where(spare > 0.0, bias_rate, jnp.where(spare < 0.0, -bias_rate, 0.0))
+        new_bias[...] = bias[...] + change
+        counts[...] = row.astype(jnp.int32)
+
+    lag_y, lag_m, lag_z = 2, 5, 10
     late = chunks - straight_chunks - 3
 
     def plain(j):
@@ -526,8 +587,10 @@
                     keep3[b, y] = down(y, j)
                     first_z(b)
 
+        pl.when(j == chunks)(tell)
+
         for lag, first, past in (
-            (lag_m, 0, late), (lag_m - 2, late, chunks - straight_chunks)
+            (lag_m, 0, late), (lag_m - 1, late, chunks - straight_chunks)
         ):
             due = jnp.logical_and(j - lag >= first, j - lag < past)
 
@@ -535,9 +598,13 @@
             def _(lag=lag):
                 merge_y(j - lag)
 
-        @pl.when(plain(j - lag_y))
+        @pl.when(jnp.logical_and(plain(j - lag_y), j - lag_y < final))
         def _():
             over_y(j - lag_y)
+
+        @pl.when(j - lag_y == final)
+        def _():
+            last_y(final)
 
         for b, special in enumerate(crossed):
 
@@ -545,7 +612,7 @@
             def _(b=b):
                 merge(b, part3, recv3, far3, mix3, s3_out, s3_in, c3_in)
 
-            @pl.when(j == special + 7)
+            @pl.when(j == special + 8)
             def _(b=b):
                 then_y(b)
 
@@ -561,11 +628,6 @@
 
     lax.fori_loop(1, chunks + lag_z, step, 0)
 
-    count = tally[...]
-    for i in range(3):
-        landed(tally_in.at[i], t_in.at[i])
-        count += tally_in[i]
-    totals[...] = count
     landed(gate_w.at[:, :, 1], m_out)
     landed(gate_w.at[:, :, 1], f_out)
     landed(tok.at[pl.ds(0, 2 * pieces - 1)], w_out.at[0])
@@ -590,13 +652,16 @@
         passed(0, zs + 1)
 
 
-def group_scratch(zs, rows, width, ff, experts):
+def group_scratch(zs, rows, top, width, ff, experts):
     slots = 2 * zs
     cd = width // chunks
     pieces = ff // lane_count
     twice = len(crossed)
     bf, f32 = jnp.bfloat16, jnp.float32
     return [
+        ((top, rows), jnp.int32),
+        ((top, rows), f32),
+        ((1, experts), f32),
         ((slots, rows, width), bf),
         ((slots, 2 * experts, rows), f32),
         ((2, pieces, 2, lane_count, width), bf),
@@ -627,19 +692,18 @@
     ]
 
 
-def finish_kernel(load, mixed, tally, bias, out, new_bias, counts, done):
-    copy = pltpu.make_async_copy(mixed, out, done)
-    copy.start()
-    experts, rows = tally.shape
-    row = lax.dot_general(
-        jnp.ones((8, rows), jnp.bfloat16), tally[...].astype(jnp.bfloat16),
-        (((1,), (1,)), ((), ())), preferred_element_type=jnp.float32,
-    )[0:1]
-    spare = load - experts * row
-    step = jnp.where(spare > 0.0, bias_rate, jnp.where(spare < 0.0, -bias_rate, 0.0))
-    new_bias[...] = bias[...] + step
-    counts[...] = row.astype(jnp.int32)
-    copy.wait()
+def finish_kernel(mixed, new_bias, counts, mixed_out, bias_out, counts_out, done):
+    rows = mixed.shape[0] // copies
+    moves = [
+        (mixed.at[pl.ds(i * rows, rows)], mixed_out.at[pl.ds(i * rows, rows)])
+        for i in range(copies)
+    ]
+    moves += [(new_bias, bias_out), (counts, counts_out)]
+    moves = [pltpu.make_async_copy(a, b, done.at[i]) for i, (a, b) in enumerate(moves)]
+    for move in moves:
+        move.start()
+    for move in moves:
+        move.wait()
 
 
 def group_body(zs, tokens, routes, route_weight, bias, w_gate, w_up, w_down):
@@ -656,47 +720,47 @@
     vmem = pl.BlockSpec(memory_space=pltpu.VMEM)
     anywhere = pl.BlockSpec(memory_space=pl.ANY)
     split = (pieces, lane_count, width)
-    mixed, totals = pl.pallas_call(
-        functools.partial(layer_kernel, zs, capacity, per_device),
+    mean_load = rows * top * lax.axis_size("dp") * lax.axis_size("expert")
+    results = pl.pallas_call(
+        functools.partial(layer_kernel, zs, capacity, per_device, mean_load),
         out_shape=(
             pltpu.VMEM((rows, width), jnp.bfloat16),
-            pltpu.VMEM((experts, rows), jnp.float32),
+            pltpu.VMEM((1, experts), jnp.float32),
+            pltpu.VMEM((1, experts), jnp.int32),
         ),
-        in_specs=[anywhere, vmem, vmem, anywhere, anywhere, anywhere],
-        out_specs=(vmem, vmem),
+        in_specs=[anywhere] * 7,
+        out_specs=(vmem, vmem, vmem),
         scratch_shapes=[
             pltpu.VMEM(shape, kind)
-            for shape, kind in group_scratch(zs, rows, width, ff, experts)
+            for shape, kind in group_scratch(zs, rows, top, width, ff, experts)
         ]
         + [
-            dma((3,)), dma, dma((slots,)), dma((2,)), dma((slots,)), dma((2,)),
+            dma((6,)), dma, dma((slots,)), dma((2,)), dma((slots,)), dma((2,)),
             dma((2, pieces)), dma((2,)), dma((chunks,)), dma, dma((2,)), dma, dma, dma,
             dma((2, pieces)), dma, dma((chunks,)), dma,
-            dma((chunks,)), dma, dma((chunks,)), dma,
-            dma((chunks,)), dma((twice,)), dma, dma((twice,)),
-            dma((twice,)), dma, dma((3,)), dma, pltpu.SemaphoreType.REGULAR,
+            dma((chunks,)), dma, dma((chunks,)), dma, dma((chunks,)),
+            dma((twice,)), dma, dma((twice,)), dma((twice,)), dma,
+            dma((zs,)), dma((3,)), dma, pltpu.SemaphoreType.REGULAR,
         ],
         compiler_params=pltpu.CompilerParams(
             collective_id=0, has_side_effects=True, vmem_limit_bytes=60000000
         ),
     )(
-        tokens, routes.T, route_weight.T,
+        tokens, routes.T, route_weight.T, bias.reshape(1, experts),
         w_gate.reshape(split), w_up.reshape(split), w_down.reshape(split),
     )
-    mixed = pltpu.with_memory_space_constraint(mixed, pltpu.VMEM)
-    totals = pltpu.with_memory_space_constraint(totals, pltpu.VMEM)
-    mean_load = rows * top * lax.axis_size("dp") * lax.axis_size("expert")
+    results = [pltpu.with_memory_space_constraint(a, pltpu.VMEM) for a in results]
     mixed, new_bias, counts = pl.pallas_call(
-        functools.partial(finish_kernel, mean_load),
+        finish_kernel,
         out_shape=(
             jax.ShapeDtypeStruct((rows, width), jnp.bfloat16),
             jax.ShapeDtypeStruct((1, experts), jnp.float32),
             jax.ShapeDtypeStruct((1, experts), jnp.int32),
         ),
         in_specs=[vmem, vmem, vmem],
-        out_specs=(anywhere, vmem, vmem),
-        scratch_shapes=[dma],
-    )(mixed, totals, bias.reshape(1, experts))
+        out_specs=(anywhere, anywhere, anywhere),
+        scratch_shapes=[dma((copies + 2,))],
+    )(*results)
     return (mixed, new_bias.reshape(experts), counts.reshape(experts))
 
 
@@ -706,7 +770,7 @@
     ff = per_device * unit
     groups = lax.axis_size("expert")
     zs = groups // 2
-    held = group_scratch(zs, rows, width, ff, bias.shape[0])
+    held = group_scratch(zs, rows, routes.shape[1], width, ff, bias.shape[0])
     total = 0
     for shape, kind in held:
         size = jnp.dtype(kind).itemsize

time: 134 us -> 130 us (0.970)
  Pallas kernels: 133 us -> 129 us
    pallas_call x2, Pallas kernels: 133 us -> 129 us  [the longest x1 128 us: group_body(): pl.pallas_call(functools.partial(layer_kernel, zs, capacity, per_device,...]
where the time goes in v3:
time: 130 us
  Pallas kernels  129 us (99%)
    pallas_call x1, Pallas kernels, group_body(): pl.pallas_call(functools.partial(layer_kernel, zs, capacity, per_device,...  128 us

profile of v3, /device:TPU:0, one launch (start us, length us, event | category | flops | bytes accessed | tf_op | source)
XLA Modules:
  0.0 129.9 jit_solution(3419518493923208432)
XLA Ops:
  0.6 128.4 %shard_map.94 = (bf16[128,2048]{1,0:T(8,128)(2,1)S(1)}, f32[1,16]{1,0:T(1,128)S(1)}, s32[1,16]{1,0:T(1,128)S(1)}) custom-call(bf16[128,2048]{1,0:T(8,128)(2,1)} %tokens.1, s32[8,128]{1,0:T(8,128)} %bitcast.11, f32[8,128]{1,0:T(8,128)} %bitcast.12, f32[1,16]{1,0:T(1,128)} %bitcast.13, bf16[3,128,2048]{2,1,0:T(8,128)(2,1)} %bitcast.8, ...), custom_call_target="tpu_custom_call" | custom-call | tf_op jit(solution)/shard_map/pallas_call | solution.py:724
  129.0 0.9 shard_map.95

commit v4 on v3

--- a/solution.py
+++ b/solution.py
@@ -12,7 +12,7 @@
 VMEM_BYTES = 67043328
 chunks = 16
 lane_count = 128
-copies = 8
+copies = 4
 crossed = (3, 6)
 straight_chunks = 1
 
@@ -351,6 +351,15 @@
     landed(down_w.at[:, 0, :, 1], md_in)
     known = 2 * ff
 
+    last_up.wait_send()
+    pl.semaphore_signal(turn, inc=1, device_id=mate, device_id_type=MESH)
+    pl.semaphore_wait(turn, 1)
+
+    def follow(j, carry):
+        cross_down(j)
+        return carry
+
+    lax.fori_loop(1, chunks, follow, 0)
     def begin(q, carry):
         near = hidden[pl.ds(q * zs, zs), :, 0:known].reshape(zs * rows, known)
         weights = down_w[0, 0].reshape(known, cd)
@@ -359,15 +368,6 @@
 
     lax.fori_loop(0, 2, begin, 0)
 
-    last_up.wait_send()
-    pl.semaphore_signal(turn, inc=1, device_id=mate, device_id_type=MESH)
-    pl.semaphore_wait(turn, 1)
-
-    def follow(j, carry):
-        cross_down(j)
-        return carry
-
-    lax.fori_loop(1, chunks, follow, 0)
     forward(1, last, up_w)
     landed(up_w.at[1, last, 1], f_in.at[1, last])
 
@@ -526,12 +526,12 @@
         value = own3[b, y] + recv4[b].astype(jnp.float32)
         out[:, span(j)] = value.astype(jnp.bfloat16)
 
+    fetch(0)
     finish(1 - y)
-    fetch(0)
     ready(0)
     away(0, down_first(1 - y))
+    fetch(1)
     finish(y)
-    fetch(1)
     keep1[0] = down_first(y)
 
     def tell():
@@ -548,7 +548,7 @@
         new_bias[...] = bias[...] + change
         counts[...] = row.astype(jnp.int32)
 
-    lag_y, lag_m, lag_z = 2, 5, 10
+    lag_y, lag_m, lag_z = 2, 5, 13
     late = chunks - straight_chunks - 3
 
     def plain(j):

time: 130 us -> 130 us (level)
  no operation moved by 1% of the time
where the time goes in v4:
time: 130 us
  Pallas kernels  129 us (99%)
    pallas_call x1, Pallas kernels, group_body(): pl.pallas_call(functools.partial(layer_kernel, zs, capacity, per_device,...  128 us

profile of v4, /device:TPU:0, one launch (start us, length us, event | category | flops | bytes accessed | tf_op | source)
XLA Modules:
  0.0 129.9 jit_solution(16448987273599549978)
XLA Ops:
  0.6 128.4 %shard_map.94 = (bf16[128,2048]{1,0:T(8,128)(2,1)S(1)}, f32[1,16]{1,0:T(1,128)S(1)}, s32[1,16]{1,0:T(1,128)S(1)}) custom-call(bf16[128,2048]{1,0:T(8,128)(2,1)} %tokens.1, s32[8,128]{1,0:T(8,128)} %bitcast.11, f32[8,128]{1,0:T(8,128)} %bitcast.12, f32[1,16]{1,0:T(1,128)} %bitcast.13, bf16[3,128,2048]{2,1,0:T(8,128)(2,1)} %bitcast.8, ...), custom_call_target="tpu_custom_call" | custom-call | tf_op jit(solution)/shard_map/pallas_call | solution.py:724
  129.0 0.8 shard_map.95
